TPU v7x, 32 devices: a whole 2x2x4 slice. The times are simulated.
32 devices in a mesh: blade: 16 (over z, y, x), span: 2 (over core).
Axes of the slice: x: 2, y: 2, z: 4, core: 2. Of those that a mesh axis runs over, the one named last changes fastest.
Arguments:
- particles: float32 [11, 32, 64, 128], P(None, 'blade', 'span')
- filled: int32 [32, 64], P('blade', 'span'), may hold values from 2 to 96, as said below
- contact_pairs: int32 [2, 32, 64, 128], P(None, 'blade', 'span'), may hold values from 0 to 639, as said below
- contact_count: int32 [32, 64], P('blade', 'span'), may hold values from 32 to 128
- movers_out: int32 [2, 2, 16, 32], P(None, None, 'blade', 'span'), may hold values from 0 to 95, as said below
- movers_in: int32 [2, 2, 16, 32], P(None, None, 'blade', 'span'), may hold values from 0 to 127, as said below
- move_count: int32 [2, 16, 2], P(None, 'blade', 'span'), may hold values from 0 to 16, as said below
Outputs:
- advanced: float32 [11, 32, 64, 128], P(None, 'blade', 'span')
Inputs may be any that keep to these rules, and one draw needn't show every extreme that they name: Live slots of a cell are its first filled ones. `contact_pairs`: every entry, counted or not, joins two live particles; direction 0 joins a slot with a higher slot of the same cell; directions never point outside the grid. The same pair may be listed more than once and then acts once per entry. `movers_out`: component 0 holds cells of the block (0 to 63), component 1 slots (below 96). Forward leavers sit in the block's last blade row, backward leavers in its first; within a device block and direction each leaver has its own cell, and each is a live slot. `movers_in`: component 0 holds cells of the block (0 to 63), component 1 slots. Arrivals from behind land in the block's first blade row, from ahead in its last; every slot is 96 or higher, and the 32 slots of one device block are all different. `move_count`: zero in the forward direction on the last blade device and in the backward direction on the first.
All inputs are finite; a program needn't handle non-finite values.
Results may differ from a plain program's by a relative error of at most 0.0001.
Values sent between devices are 32-bit elements; how exact they have to be, the bound alone decides.
A program may use at most 64 MiB of HBM per device.

v0:
```python
import functools

import jax
import jax.numpy as jnp
from jax import lax
from jax.experimental import pallas as pl
from jax.experimental.pallas import tpu as pltpu
from jax.sharding import PartitionSpec as P

spring = 4.0
normal_damp = 0.5
tangent_damp = 0.3
conduct = 40.0
timestep_length = 0.05
density = 100.0
gravity = 9.81
soft_len = 0.05
row_steps = (0, 1, 0, 1, 1)
col_steps = (0, 0, 1, 1, -1)
MESH = pl.DeviceIdType.MESH
TILE = 8


def cross(a, b):
    return (
        a[1] * b[2] - a[2] * b[1],
        a[2] * b[0] - a[0] * b[2],
        a[0] * b[1] - a[1] * b[0],
    )


def lanes_of(table, index):
    return jnp.take_along_axis(table, index, axis=1, mode="promise_in_bounds")


def pair_terms(first, second, row_shift, col_shift, live):
    gap = (
        second[0] + row_shift - first[0],
        second[1] + col_shift - first[1],
        second[2] - first[2],
    )
    distance = jnp.sqrt(gap[0] * gap[0] + gap[1] * gap[1] + gap[2] * gap[2] + soft_len * soft_len)
    inverse = 1.0 / distance
    normal = tuple(g * inverse for g in gap)
    rad_first, rad_second = first[9], second[9]
    intersection = rad_first + rad_second - distance
    spin = tuple(rad_first * first[6 + c] + rad_second * second[6 + c] for c in range(3))
    turn = cross(spin, normal)
    relative = tuple(second[3 + c] - first[3 + c] - turn[c] for c in range(3))
    speed = relative[0] * normal[0] + relative[1] * normal[1] + relative[2] * normal[2]
    friction = tuple(tangent_damp * (relative[c] - speed * normal[c]) for c in range(3))
    push = normal_damp * speed - spring * intersection
    force = tuple(push * normal[c] + friction[c] for c in range(3))
    torque = cross(normal, friction)
    denom = jnp.where(live, rad_first + rad_second, 1.0)
    heat = 2.0 * conduct * rad_first * rad_second / denom * (second[10] - first[10])
    on_first = force + tuple(rad_first * t for t in torque) + (heat,)
    on_second = tuple(-f for f in force) + tuple(rad_second * t for t in torque) + (-heat,)
    keep = lambda v: jnp.where(live, v, 0.0)
    return [keep(v) for v in on_first], [keep(v) for v in on_second]


def kernel(
    shape,
    blades,
    spans,
    parts_hbm,
    filled_hbm,
    pairs_hbm,
    count_hbm,
    out_movers_hbm,
    in_movers_hbm,
    move_count_hbm,
    out_ref,
    ghost,
    pairs_ref,
    count_own,
    count_prev,
    filled_ref,
    out_movers,
    in_movers,
    move_count,
    first_terms,
    second_terms,
    count_wide,
    filled_wide,
    totals,
    owed_low,
    owed_high,
    msg_out,
    msg_in,
    local_sem,
    send_sem,
    recv_sem,
):
    components, rows, cols, slots = shape
    movers = out_movers.shape[3]
    wide = cols + 2
    i = lax.axis_index("blade")
    j = lax.axis_index("span")
    has = {}
    for di in (-1, 0, 1):
        for dj in (-1, 0, 1):
            if (di, dj) != (0, 0):
                a, b = i + di, j + dj
                has[di, dj] = (a >= 0) & (a < blades) & (b >= 0) & (b < spans)

    own_cols = slice(TILE, TILE + cols)
    own = [
        pltpu.make_async_copy(source, target, local_sem.at[n])
        for n, (source, target) in enumerate(
            (
                (count_hbm, count_own),
                (filled_hbm, filled_ref),
                (pairs_hbm, pairs_ref.at[:, 1 : rows + 1]),
                (parts_hbm, ghost.at[:, 1 : rows + 1, own_cols, :]),
                (out_movers_hbm, out_movers),
                (in_movers_hbm, in_movers),
                (move_count_hbm, move_count),
            )
        )
    ]
    barrier = pltpu.get_barrier_semaphore()
    expected = jnp.int32(0)
    for (di, dj), there in has.items():
        expected = expected + there.astype(jnp.int32)

        @pl.when(there)
        def _(di=di, dj=dj):
            pl.semaphore_signal(
                barrier, inc=1, device_id=(i + di, j + dj), device_id_type=MESH
            )

    for copy in own:
        copy.start()
    pl.semaphore_wait(barrier, expected)

    def remote(which, source, target, di, dj):
        return pltpu.make_async_remote_copy(
            src_ref=source,
            dst_ref=target,
            send_sem=send_sem.at[which],
            recv_sem=recv_sem.at[which],
            device_id=(i + di, j + dj),
            device_id_type=MESH,
        )

    low = slice(0, 1)
    high = slice(cols - 1, cols)
    left = slice(TILE - 1, TILE)
    right = slice(TILE + cols, TILE + cols + 1)
    last = slice(rows - 1, rows)
    after = slice(rows + 1, rows + 2)
    moves = (
        (parts_hbm.at[:, 0:1], ghost.at[:, after, own_cols, :], -1, 0),
        (parts_hbm.at[:, :, low, :], ghost.at[:, 1 : rows + 1, right, :], 0, -1),
        (parts_hbm.at[:, :, high, :], ghost.at[:, 1 : rows + 1, left, :], 0, 1),
        (parts_hbm.at[:, 0:1, low, :], ghost.at[:, after, right, :], -1, -1),
        (parts_hbm.at[:, 0:1, high, :], ghost.at[:, after, left, :], -1, 1),
        (parts_hbm.at[:, last], ghost.at[:, 0:1, own_cols, :], 1, 0),
        (pairs_hbm.at[:, last], pairs_ref.at[:, 0:1], 1, 0),
        (count_hbm, count_prev, 1, 0),
        (totals.at[1:rows, wide - 1], owed_low.at[1:rows], 0, 1),
        (totals.at[1:rows, 0], owed_high.at[1:rows], 0, -1),
        (msg_out.at[0], msg_in.at[0], 1, 0),
        (msg_out.at[1], msg_in.at[1], -1, 0),
        (totals.at[0:1, wide - 1], owed_low.at[0:1], 0, 1),
        (totals.at[0:1, 0], owed_high.at[0:1], 0, -1),
    )
    copies = [
        (remote(n, source, target, di, dj), di, dj)
        for n, (source, target, di, dj) in enumerate(moves)
    ]

    def start(*which):
        for w in which:
            copy, di, dj = copies[w]

            @pl.when(has[di, dj])
            def _(copy=copy):
                copy.start()

    def arrive(*which):
        for w in which:
            copy, di, dj = copies[w]

            @pl.when(has[-di, -dj])
            def _(copy=copy):
                copy.wait_recv()

    def sent(*which):
        for w in which:
            copy, di, dj = copies[w]

            @pl.when(has[di, dj])
            def _(copy=copy):
                copy.wait_send()

    start(1, 2, 3, 4, 7, 6, 5, 0)

    diagonal = lax.broadcasted_iota(jnp.int32, (cols, cols), 0) == lax.broadcasted_iota(
        jnp.int32, (cols, cols), 1
    )

    def spread(source, r, target, at):
        line = jnp.broadcast_to(source[r : r + 1, :].astype(jnp.float32), (cols, cols))
        column = jnp.sum(jnp.where(diagonal, line, 0.0), axis=1, keepdims=True)
        target[at] = jnp.broadcast_to(column, (cols, slots))

    def clear(n, _):
        for r in range(rows):
            totals[r, n] = jnp.zeros((8, slots), jnp.float32)
        return 0

    lax.fori_loop(0, wide, clear, 0)
    lane = lax.broadcasted_iota(jnp.int32, (TILE, slots), 1)
    lane_f = lane.astype(jnp.float32)
    groups = cols // TILE

    def force_row(r, headings):
        def group(g, _):
            at = pl.multiple_of(g * TILE, TILE)
            ids = pairs_ref[0, r, pl.ds(at, TILE), :]
            code = pairs_ref[1, r, pl.ds(at, TILE), :]
            heading = code // slots
            target = code - heading * slots
            live = lane_f < count_wide[r, pl.ds(at, TILE), :]
            ids = jnp.clip(ids, 0, slots - 1)
            first = [
                lanes_of(ghost[c, r, pl.ds(at + TILE, TILE), :], ids) for c in range(components)
            ]
            second = [None] * components
            for n, d in enumerate(headings):
                pick = heading == d
                for c in range(components):
                    rows_at = pl.ds(at + TILE + col_steps[d], TILE)
                    value = lanes_of(ghost[c, r + row_steps[d], rows_at, :], target)
                    second[c] = value if n == 0 else jnp.where(pick, value, second[c])
            row_shift = jnp.where((heading == 0) | (heading == 2), 0.0, 1.0)
            col_shift = jnp.where(
                (heading == 2) | (heading == 3), 1.0, jnp.where(heading == 4, -1.0, 0.0)
            )
            on_first, on_second = pair_terms(first, second, row_shift, col_shift, live)
            zero = jnp.zeros((TILE, slots), jnp.float32)
            base = (r * cols + g * TILE) * 8
            for c, (a, b) in enumerate(zip(on_first + [zero], on_second + [zero])):
                first_terms[pl.ds(base + c, TILE, stride=8), :] = a
                second_terms[pl.ds(base + c, TILE, stride=8), :] = b
            return 0

        lax.fori_loop(0, groups, group, 0)

    slot_ids = lax.broadcasted_iota(jnp.int32, (slots, slots), 0)

    def scatter_row(r, near_too, headings):
        count = len(headings) * 8

        def group(g, _):
            at = pl.multiple_of(g * TILE, TILE)
            ids = pairs_ref[0, r, pl.ds(at, TILE), :]
            code = pairs_ref[1, r, pl.ds(at, TILE), :]
            heading = code // slots
            target = code - heading * slots
            for n in range(TILE):
                base = pl.multiple_of((r * cols + g * TILE + n) * 8, 8)
                b = second_terms[pl.ds(base, 8), :]
                head = heading[n : n + 1]
                terms = jnp.concatenate(
                    [jnp.where(head == d, b, 0.0) for d in headings], axis=0
                )
                hot = jnp.where(slot_ids == target[n : n + 1], 1.0, 0.0)
                if near_too:
                    a = first_terms[pl.ds(base, 8), :]
                    zero = jnp.zeros((8, slots), jnp.float32)
                    near = jnp.concatenate([a] + [zero] * (len(headings) - 1), axis=0)
                    terms = jnp.concatenate([near, terms], axis=1)
                    near_hot = jnp.where(slot_ids == ids[n : n + 1], 1.0, 0.0)
                    hot = jnp.concatenate([near_hot, hot], axis=1)
                coarse = terms.astype(jnp.bfloat16).astype(jnp.float32)
                split = jnp.concatenate([coarse, terms - coarse], axis=0).astype(jnp.bfloat16)
                summed = lax.dot_general(
                    split,
                    hot.astype(jnp.bfloat16),
                    (((1,), (1,)), ((), ())),
                    preferred_element_type=jnp.float32,
                )
                summed = summed[:count] + summed[count:]
                for m, d in enumerate(headings):
                    col = g * TILE + n + 1 + col_steps[d]
                    totals[r - 1 + row_steps[d], col] += summed[m * 8 : m * 8 + 8]
            return 0

        lax.fori_loop(0, groups, group, 0)

    def step_row(r):
        for g in range(groups):
            cells = slice(g * TILE, (g + 1) * TILE)
            sums = []
            for c in range(7):
                s = totals[r, 1 + g * TILE : 1 + (g + 1) * TILE, c, :]
                sums.append(s)
            live = lane_f < filled_wide[r, cells, :]
            state = [ghost[c, r + 1, TILE + g * TILE : TILE + (g + 1) * TILE, :] for c in range(components)]
            safe = jnp.where(live, state[9], 1.0)
            mass = density * safe * safe * safe
            inverse = 1.0 / mass
            spin_inverse = 1.0 / (0.4 * mass * safe * safe)
            keep = lambda v: jnp.where(live, v, 0.0)
            for c in range(3):
                accel = sums[c] * inverse
                if c == 2:
                    accel = accel - gravity
                speed = state[3 + c] + timestep_length * accel
                out_ref[c, r, cells, :] = keep(state[c] + timestep_length * speed)
                out_ref[3 + c, r, cells, :] = keep(speed)
                out_ref[6 + c, r, cells, :] = keep(
                    state[6 + c] + timestep_length * sums[3 + c] * spin_inverse
                )
            out_ref[9, r, cells, :] = keep(state[9])
            out_ref[10, r, cells, :] = keep(state[10] + timestep_length * sums[6] * inverse)

    line_lane = lax.broadcasted_iota(jnp.int32, (1, slots), 1)
    cell_ids = lax.broadcasted_iota(jnp.int32, (cols, slots), 0)
    lane_ids = lax.broadcasted_iota(jnp.int32, (cols, slots), 1)

    def leave(direction, r):
        cell_line = jnp.full((1, slots), -1, jnp.int32)
        slot_line = jnp.zeros((1, slots), jnp.int32)
        for k in range(movers):
            cell_line = jnp.where(line_lane == k, out_movers[direction, 0, 0, k] - r * cols, cell_line)
            slot_line = jnp.where(line_lane == k, out_movers[direction, 1, 0, k], slot_line)
        moving = line_lane < move_count[0, 0, direction]
        chosen = (cell_ids == cell_line) & moving
        slot_f = jnp.where(chosen, jnp.broadcast_to(slot_line + 1, (cols, slots)).astype(jnp.float32), 0.0)
        slot_of = jnp.sum(slot_f, axis=1, keepdims=True).astype(jnp.int32) - 1
        slot_of = jnp.broadcast_to(slot_of, (cols, slots))
        leaving = lane_ids == slot_of
        index = jnp.maximum(slot_of, 0)
        shift = jnp.where(moving, -1.0 if direction == 0 else 1.0, 0.0)
        for c in range(components):
            value = out_ref[c, r]
            spread = lanes_of(value, index)
            line = jnp.sum(jnp.where(chosen, spread, 0.0), axis=0, keepdims=True)
            if c == 0:
                line = line + shift
            msg_out[direction, c : c + 1, :] = line
            out_ref[c, r] = jnp.where(leaving, 0.0, value)

    def put(direction, r, there):
        key = jnp.zeros((1, slots), jnp.int32)
        cell_line = jnp.full((1, slots), -1, jnp.int32)
        for k in range(movers):
            hit = line_lane == in_movers[direction, 1, 0, k]
            key = jnp.where(hit, k, key)
            cell_line = jnp.where(hit, in_movers[direction, 0, 0, k] - r * cols, cell_line)
        cell_line = jnp.where(there, cell_line, -1)
        landing = cell_ids == cell_line
        key = jnp.broadcast_to(key, (msg_in.shape[1], slots))
        values = lanes_of(msg_in[direction], key)
        for c in range(components):
            out_ref[c, r] = jnp.where(landing, values[c : c + 1], out_ref[c, r])

    every, inside, across = (0, 1, 2, 3, 4), (0, 2), (1, 3, 4)
    for c in range(msg_out.shape[1] - components):
        for d in range(2):
            msg_out[d, components + c : components + c + 1, :] = jnp.zeros((1, slots), jnp.float32)
    for copy in own:
        copy.wait()
    for r in range(rows):
        spread(count_own, r, count_wide, r + 1)
        spread(filled_ref, r, filled_wide, r)
    arrive(1, 2)
    for r in range(1, rows):
        force_row(r, every)
        scatter_row(r, True, every)
    arrive(7, 6, 5)
    spread(count_prev, rows - 1, count_wide, 0)
    count_wide[0] = jnp.where(has[-1, 0], count_wide[0], 0.0)
    force_row(0, across)
    scatter_row(0, False, across)
    arrive(3, 4, 0)
    force_row(rows, every)
    scatter_row(rows, True, inside)
    start(8, 9, 12, 13)
    arrive(8, 9)

    def add_owed(r):
        totals[r, 1] += jnp.where(has[0, -1], owed_low[r], 0.0)
        totals[r, cols] += jnp.where(has[0, 1], owed_high[r], 0.0)

    for r in range(1, rows):
        add_owed(r)
        step_row(r)
    if rows > 1:
        leave(0, rows - 1)
        start(10)
    arrive(12, 13)
    add_owed(0)
    step_row(0)
    if rows == 1:
        leave(0, 0)
        start(10)
    leave(1, 0)
    start(11)
    sent(*range(10), 12, 13)
    arrive(10)
    put(0, 0, has[-1, 0])
    arrive(11)
    put(1, rows - 1, has[1, 0])
    sent(10, 11)


def body(blades, spans, particles, filled, contact_pairs, contact_count, movers_out, movers_in, move_count):
    components, rows, cols, slots = particles.shape
    padded = -(-components // 8) * 8
    f32, i32 = jnp.float32, jnp.int32
    remote_copies = 14
    return pl.pallas_call(
        functools.partial(kernel, particles.shape, blades, spans),
        out_shape=jax.ShapeDtypeStruct(particles.shape, f32),
        in_specs=[pl.BlockSpec(memory_space=pl.ANY)] * 7,
        out_specs=pl.BlockSpec(memory_space=pltpu.VMEM),
        scratch_shapes=[
            pltpu.VMEM((components, rows + 2, cols + 2 * TILE, slots), f32),
            pltpu.VMEM((2, rows + 1, cols, contact_pairs.shape[3]), i32),
            pltpu.VMEM((rows, cols), i32),
            pltpu.VMEM((rows, cols), i32),
            pltpu.VMEM((rows, cols), i32),
            pltpu.SMEM(movers_out.shape, i32),
            pltpu.SMEM(movers_in.shape, i32),
            pltpu.SMEM((1, 1, 2), i32),
            pltpu.VMEM(((rows + 1) * cols * 8, slots), f32),
            pltpu.VMEM(((rows + 1) * cols * 8, slots), f32),
            pltpu.VMEM((rows + 1, cols, slots), f32),
            pltpu.VMEM((rows, cols, slots), f32),
            pltpu.VMEM((rows, cols + 2, 8, slots), f32),
            pltpu.VMEM((rows, 8, slots), f32),
            pltpu.VMEM((rows, 8, slots), f32),
            pltpu.VMEM((2, padded, slots), f32),
            pltpu.VMEM((2, padded, slots), f32),
            pltpu.SemaphoreType.DMA((7,)),
            pltpu.SemaphoreType.DMA((remote_copies,)),
            pltpu.SemaphoreType.DMA((remote_copies,)),
        ],
        compiler_params=pltpu.CompilerParams(collective_id=0, has_side_effects=True),
    )(
        particles,
        filled,
        contact_pairs,
        contact_count,
        movers_out,
        movers_in,
        jnp.transpose(move_count, (1, 2, 0)),
    )


def solution(mesh):
    sizes = dict(mesh.shape)
    return jax.shard_map(
        functools.partial(body, sizes["blade"], sizes["span"]),
        mesh=mesh,
        in_specs=(
            P(None, "blade", "span", None),
            P("blade", "span"),
            P(None, "blade", "span", None),
            P("blade", "span"),
            P(None, None, "blade", "span"),
            P(None, None, "blade", "span"),
            P(None, "blade", "span"),
        ),
        out_specs=P(None, "blade", "span", None),
        check_vma=False,
    )
```

profile of v0, /device:TPU:0, one launch (start us, length us, event | category | flops | bytes accessed | tf_op | source)
XLA Modules:
  0.0 23.8 jit_solution(763572384230329524)
XLA Ops:
  0.0 22.0 %shard_map.73 = f32[11,2,32,128]{3,2,1,0:T(8,128)} custom-call(f32[11,2,32,128]{3,2,1,0:T(8,128)} %parts_hbm.1, s32[2,32]{1,0:T(2,128)} %filled_hbm.1, s32[2,2,32,128]{3,2,1,0:T(8,128)} %pairs_hbm.1, s32[2,32]{1,0:T(2,128)} %count_hbm.1, s32[2,2,1,16]{3,2,1,0:T(1,128)} %out_movers_hbm.1, s32[2,2,1,16]{3,2,1,0:T(1,128)} %in_movers_hbm.1, s32[1,1,2]{2,1,0:T(1,128)} %bitcast.1), custom_call_target="tpu_custom_call" | custom-call | tf_op jit(solution)/shard_map/pallas_call | solution.py:418
  22.0 1.7 %copy.9 = f32[11,2,32,128]{3,2,1,0:T(8,128)} copy(f32[11,2,32,128]{3,2,1,0:T(8,128)} %shard_map.73) | data formatting | bytes 720896
where the time goes:
time: 23.9 us; the launch traced here: 23.8 us
  Pallas kernels  22 us (92%)
  local copies, waits for them, and re-layouts  1.74 us (7%)
    pallas_call x1, Pallas kernels, body(): pl.pallas_call(functools.partial(kernel, particles.shape, blades, spans),...  22 us
    unnamed x1, local copies, waits for them, and re-layouts  1.74 us

commit v1 on v0

--- a/solution.py
+++ b/solution.py
@@ -19,6 +19,7 @@
 col_steps = (0, 0, 1, 1, -1)
 MESH = pl.DeviceIdType.MESH
 TILE = 8
+VMEM_GRANT = 16 << 20
 
 
 def cross(a, b):
@@ -417,7 +418,7 @@
     remote_copies = 14
     return pl.pallas_call(
         functools.partial(kernel, particles.shape, blades, spans),
-        out_shape=jax.ShapeDtypeStruct(particles.shape, f32),
+        out_shape=pltpu.VMEM(particles.shape, f32),
         in_specs=[pl.BlockSpec(memory_space=pl.ANY)] * 7,
         out_specs=pl.BlockSpec(memory_space=pltpu.VMEM),
         scratch_shapes=[
@@ -442,15 +443,20 @@
             pltpu.SemaphoreType.DMA((remote_copies,)),
             pltpu.SemaphoreType.DMA((remote_copies,)),
         ],
-        compiler_params=pltpu.CompilerParams(collective_id=0, has_side_effects=True),
+        compiler_params=pltpu.CompilerParams(collective_id=0, has_side_effects=True, vmem_limit_bytes=VMEM_GRANT),
     )(
-        particles,
-        filled,
-        contact_pairs,
-        contact_count,
-        movers_out,
-        movers_in,
-        jnp.transpose(move_count, (1, 2, 0)),
+        *(
+            pltpu.with_memory_space_constraint(x, pltpu.HBM)
+            for x in (
+                particles,
+                filled,
+                contact_pairs,
+                contact_count,
+                movers_out,
+                movers_in,
+                jnp.transpose(move_count, (1, 2, 0)),
+            )
+        )
     )
 
 

time: 23.9 us -> 22.2 us (0.929)
  local copies, waits for them, and re-layouts: 1.74 us -> 0.74 us
  Pallas kernels: 22 us -> 21.3 us
    unnamed x1, local copies, waits for them, and re-layouts: 1.74 us -> 0.74 us
    pallas_call x1, Pallas kernels: 22 us -> 21.3 us  [body(): pl.pallas_call(functools.partial(kernel, particles.shape, blades, spans),...]
where the time goes in v1:
time: 22.2 us; the launch traced here: 22 us
  Pallas kernels  21.3 us (96%)
  local copies, waits for them, and re-layouts  0.74 us (3%)
    pallas_call x1, Pallas kernels, body(): pl.pallas_call(functools.partial(kernel, particles.shape, blades, spans),...  21.3 us
    unnamed x1, local copies, waits for them, and re-layouts  0.74 us

profile of v1, /device:TPU:0, one launch (start us, length us, event | category | flops | bytes accessed | tf_op | source)
XLA Modules:
  0.0 22.0 jit_solution(17615310344898952342)
XLA Ops:
  0.0 21.3 %shard_map.73 = f32[11,2,32,128]{3,2,1,0:T(8,128)S(1)} custom-call(f32[11,2,32,128]{3,2,1,0:T(8,128)} %parts_hbm.1, s32[2,32]{1,0:T(2,128)} %filled_hbm.1, s32[2,2,32,128]{3,2,1,0:T(8,128)} %pairs_hbm.1, s32[2,32]{1,0:T(2,128)} %count_hbm.1, s32[2,2,1,16]{3,2,1,0:T(1,128)} %out_movers_hbm.1, s32[2,2,1,16]{3,2,1,0:T(1,128)} %in_movers_hbm.1, s32[1,1,2]{2,1,0:T(1,128)} %bitcast.1), custom_call_target="tpu_custom_call" | custom-call | tf_op jit(solution)/shard_map/pallas_call | solution.py:419
  21.3 0.7 %copy.9 = f32[11,2,32,128]{3,2,1,0:T(8,128)} copy(f32[11,2,32,128]{3,2,1,0:T(8,128)S(1)} %shard_map.73) | data formatting | bytes 720896

commit v2 on v1

v2 whole, which is shorter than its diff:
```python
import functools

import jax
import jax.numpy as jnp
from jax import lax
from jax.experimental import pallas as pl
from jax.experimental.pallas import tpu as pltpu
from jax.sharding import PartitionSpec as P

spring = 4.0
normal_damp = 0.5
tangent_damp = 0.3
conduct = 40.0
timestep_length = 0.05
density = 100.0
gravity = 9.81
soft_len = 0.05
row_steps = (0, 1, 0, 1, 1)
col_steps = (0, 0, 1, 1, -1)
MESH = pl.DeviceIdType.MESH
TILE = 8
VMEM_GRANT = 16 << 20


def cross(a, b):
    return (
        a[1] * b[2] - a[2] * b[1],
        a[2] * b[0] - a[0] * b[2],
        a[0] * b[1] - a[1] * b[0],
    )


def lanes_of(table, index):
    return jnp.take_along_axis(table, index, axis=1, mode="promise_in_bounds")


def pair_terms(first, second, row_shift, col_shift, live):
    gap = (
        second[0] + row_shift - first[0],
        second[1] + col_shift - first[1],
        second[2] - first[2],
    )
    distance = jnp.sqrt(gap[0] * gap[0] + gap[1] * gap[1] + gap[2] * gap[2] + soft_len * soft_len)
    inverse = 1.0 / distance
    normal = tuple(g * inverse for g in gap)
    rad_first, rad_second = first[9], second[9]
    intersection = rad_first + rad_second - distance
    spin = tuple(rad_first * first[6 + c] + rad_second * second[6 + c] for c in range(3))
    turn = cross(spin, normal)
    relative = tuple(second[3 + c] - first[3 + c] - turn[c] for c in range(3))
    speed = relative[0] * normal[0] + relative[1] * normal[1] + relative[2] * normal[2]
    friction = tuple(tangent_damp * (relative[c] - speed * normal[c]) for c in range(3))
    push = normal_damp * speed - spring * intersection
    force = tuple(push * normal[c] + friction[c] for c in range(3))
    torque = cross(normal, friction)
    denom = jnp.where(live, rad_first + rad_second, 1.0)
    heat = 2.0 * conduct * rad_first * rad_second / denom * (second[10] - first[10])
    on_first = force + tuple(rad_first * t for t in torque) + (heat,)
    on_second = tuple(-f for f in force) + tuple(rad_second * t for t in torque) + (-heat,)
    keep = lambda v: jnp.where(live, v, 0.0)
    return [keep(v) for v in on_first], [keep(v) for v in on_second]


def chunks_of(cols):
    ghost_cuts = [0] + [n + 1 for n in range(TILE, cols, TILE)] + [cols]
    owed_cuts = [0] + [n - 1 for n in range(TILE, cols, TILE)] + [cols]
    return list(zip(ghost_cuts, ghost_cuts[1:])), list(zip(owed_cuts, owed_cuts[1:]))


def packing(components, slots, movers):
    live = slots - 2 * movers
    spare = slots - live
    pieces = live // spare
    riders = components // (pieces + 1) if live % spare == 0 else 0
    return live, spare, pieces, riders


def kernel(
    shape,
    blades,
    spans,
    parts_hbm,
    filled_hbm,
    pairs_hbm,
    count_hbm,
    out_movers_hbm,
    in_movers_hbm,
    move_count_hbm,
    out_ref,
    ghost,
    packed,
    pairs_ref,
    count_own,
    filled_ref,
    out_movers,
    in_movers,
    move_count,
    first_terms,
    second_terms,
    count_wide,
    filled_wide,
    totals,
    edge_out,
    owed_low,
    owed_high,
    late_low,
    late_high,
    owed,
    owed_diag,
    msg_out,
    msg_in,
    landed,
    local_sem,
    send_sem,
    recv_sem,
):
    components, rows, cols, slots = shape
    movers = out_movers.shape[3]
    wide = cols + 2
    groups = cols // TILE
    live_slots, spare, pieces, riders = packing(components, slots, movers)
    carried = components - riders
    ghost_chunks, owed_chunks = chunks_of(cols)
    i = lax.axis_index("blade")
    j = lax.axis_index("span")
    has = {}
    for di in (-1, 0, 1):
        for dj in (-1, 0, 1):
            if (di, dj) != (0, 0):
                a, b = i + di, j + dj
                has[di, dj] = (a >= 0) & (a < blades) & (b >= 0) & (b < spans)

    own_cols = slice(TILE, TILE + cols)
    own = [
        pltpu.make_async_copy(source, target, local_sem.at[n])
        for n, (source, target) in enumerate(
            (
                (parts_hbm.at[:, 0], ghost.at[:, 0, own_cols, :]),
                (count_hbm, count_own),
                (filled_hbm, filled_ref),
                (pairs_hbm, pairs_ref),
                (parts_hbm.at[:, 1:rows], ghost.at[:, 1:rows, own_cols, :]),
                (out_movers_hbm, out_movers),
                (in_movers_hbm, in_movers),
                (move_count_hbm, move_count),
            )
        )
    ]
    barrier = pltpu.get_barrier_semaphore()
    expected = jnp.int32(0)
    for (di, dj), there in has.items():
        expected = expected + there.astype(jnp.int32)

        @pl.when(there)
        def _(di=di, dj=dj):
            pl.semaphore_signal(
                barrier, inc=1, device_id=(i + di, j + dj), device_id_type=MESH
            )

    for copy in own:
        copy.start()

    moves = {}

    def move(name, source, target, di, dj):
        n = len(moves)
        copy = pltpu.make_async_remote_copy(
            src_ref=source,
            dst_ref=target,
            send_sem=send_sem.at[n],
            recv_sem=recv_sem.at[n],
            device_id=(i + di, j + dj),
            device_id_type=MESH,
        )
        moves[name] = (copy, di, dj)

    low = slice(0, 1)
    high = slice(cols - 1, cols)
    left = slice(TILE - 1, TILE)
    right = slice(TILE + cols, TILE + cols + 1)
    for n, (a, b) in enumerate(ghost_chunks):
        target = ghost.at[0:carried, rows, TILE + a : TILE + b, :]
        move(("ghost", n), packed.at[:, a:b], target, -1, 0)
    move("corner right", parts_hbm.at[:, 0, low, :], ghost.at[:, rows, right, :], -1, -1)
    move("corner left", parts_hbm.at[:, 0, high, :], ghost.at[:, rows, left, :], -1, 1)
    move("side right", parts_hbm.at[:, :, low, :], ghost.at[:, 0:rows, right, :], 0, -1)
    move("side left", parts_hbm.at[:, :, high, :], ghost.at[:, 0:rows, left, :], 0, 1)
    move("edge low", edge_out.at[1], owed_low, 0, 1)
    move("edge high", edge_out.at[0], owed_high, 0, -1)
    move("late low", totals.at[rows, wide - 1], late_low, 0, 1)
    move("late high", totals.at[rows, 0], late_high, 0, -1)
    for n, (a, b) in enumerate(owed_chunks):
        move(("owed", n), totals.at[rows, 1 + a : 1 + b], owed.at[a:b], 1, 0)
    move("diag low", totals.at[rows, wide - 1], owed_diag.at[0], 1, 1)
    move("diag high", totals.at[rows, 0], owed_diag.at[1], 1, -1)
    move("forward", msg_out.at[0], msg_in.at[0], 1, 0)
    move("backward", msg_out.at[1], msg_in.at[1], -1, 0)

    def start(*which):
        for w in which:
            copy, di, dj = moves[w]

            @pl.when(has[di, dj])
            def _(copy=copy):
                copy.start()

    def arrive(*which):
        for w in which:
            copy, di, dj = moves[w]

            @pl.when(has[-di, -dj])
            def _(copy=copy):
                copy.wait_recv()

    def sent(*which):
        for w in which:
            copy, di, dj = moves[w]

            @pl.when(has[di, dj])
            def _(copy=copy):
                copy.wait_send()

    diagonal = lax.broadcasted_iota(jnp.int32, (cols, cols), 0) == lax.broadcasted_iota(
        jnp.int32, (cols, cols), 1
    )
    lane = lax.broadcasted_iota(jnp.int32, (TILE, slots), 1)
    lane_f = lane.astype(jnp.float32)
    slot_ids = lax.broadcasted_iota(jnp.int32, (slots, slots), 0)
    line_lane = lax.broadcasted_iota(jnp.int32, (1, slots), 1)
    cell_ids = lax.broadcasted_iota(jnp.int32, (cols, slots), 0)
    lane_ids = lax.broadcasted_iota(jnp.int32, (cols, slots), 1)

    def spread(source, r, target, at):
        line = jnp.broadcast_to(source[r : r + 1, :].astype(jnp.float32), (cols, cols))
        column = jnp.sum(jnp.where(diagonal, line, 0.0), axis=1, keepdims=True)
        target[at] = jnp.broadcast_to(column, (cols, slots))

    def clear(n, _):
        for r in range(rows + 1):
            totals[r, n] = jnp.zeros((8, slots), jnp.float32)
        return 0

    def pack():
        for c in range(carried):
            value = ghost[c, 0, own_cols, :]
            if c < riders * pieces:
                rider, piece = carried + c // pieces, c % pieces
                shift = live_slots - piece * spare
                moved = pltpu.roll(ghost[rider, 0, own_cols, :], shift, 1)
                value = jnp.where(lane_ids < live_slots, value, moved)
            packed[c] = value

    def unpack(at):
        for e in range(riders):
            value = None
            for piece in range(pieces):
                shift = (piece * spare - live_slots) % slots
                moved = pltpu.roll(ghost[e * pieces + piece, rows, TILE + at : 2 * TILE + at, :], shift, 1)
                value = moved if piece == 0 else jnp.where(lane >= piece * spare, moved, value)
            ghost[carried + e, rows, TILE + at : 2 * TILE + at, :] = value

    def tiles_of(g):
        return g * TILE if isinstance(g, int) else pl.multiple_of(g * TILE, TILE)

    def contacts_of(r, g):
        at = tiles_of(g)
        ids = pairs_ref[0, r, pl.ds(at, TILE), :]
        code = pairs_ref[1, r, pl.ds(at, TILE), :]
        heading = code // slots
        return ids, heading, code - heading * slots

    def forces(r, g, headings):
        at = tiles_of(g)
        ids, heading, target = contacts_of(r, g)
        live = lane_f < count_wide[r, pl.ds(at, TILE), :]
        first = [
            lanes_of(ghost[c, r, pl.ds(at + TILE, TILE), :], ids) for c in range(components)
        ]
        second = [None] * components
        for n, d in enumerate(headings):
            pick = heading == d
            for c in range(components):
                rows_at = pl.ds(at + TILE + col_steps[d], TILE)
                value = lanes_of(ghost[c, r + row_steps[d], rows_at, :], target)
                second[c] = value if n == 0 else jnp.where(pick, value, second[c])
        row_shift = jnp.where((heading == 0) | (heading == 2), 0.0, 1.0)
        col_shift = jnp.where(
            (heading == 2) | (heading == 3), 1.0, jnp.where(heading == 4, -1.0, 0.0)
        )
        on_first, on_second = pair_terms(first, second, row_shift, col_shift, live)
        zero = jnp.zeros((TILE, slots), jnp.float32)
        base = (r * cols + g * TILE) * 8
        for c, (a, b) in enumerate(zip(on_first + [zero], on_second + [zero])):
            first_terms[pl.ds(base + c, TILE, stride=8), :] = a
            second_terms[pl.ds(base + c, TILE, stride=8), :] = b

    def summed_of(r, g, n, contacts, headings, near_too):
        ids, heading, target = contacts
        base = (r * cols + g * TILE + n) * 8
        if not isinstance(base, int):
            base = pl.multiple_of(base, 8)
        b = second_terms[pl.ds(base, 8), :]
        head = heading[n : n + 1]
        terms = jnp.concatenate([jnp.where(head == d, b, 0.0) for d in headings], axis=0)
        hot = jnp.where(slot_ids == target[n : n + 1], 1.0, 0.0)
        if near_too:
            a = first_terms[pl.ds(base, 8), :]
            zero = jnp.zeros((8, slots), jnp.float32)
            near = jnp.concatenate([a] + [zero] * (len(headings) - 1), axis=0)
            terms = jnp.concatenate([near, terms], axis=1)
            near_hot = jnp.where(slot_ids == ids[n : n + 1], 1.0, 0.0)
            hot = jnp.concatenate([near_hot, hot], axis=1)
        coarse = terms.astype(jnp.bfloat16).astype(jnp.float32)
        split = jnp.concatenate([coarse, terms - coarse], axis=0).astype(jnp.bfloat16)
        summed = lax.dot_general(
            split,
            hot.astype(jnp.bfloat16),
            (((1,), (1,)), ((), ())),
            preferred_element_type=jnp.float32,
        )
        count = len(headings) * 8
        return summed[:count] + summed[count:]

    every = (0, 1, 2, 3, 4)

    def scatter(r, g):
        contacts = contacts_of(r, g)
        for n in range(TILE):
            summed = summed_of(r, g, n, contacts, every, True)
            for m, d in enumerate(every):
                col = g * TILE + n + 1 + col_steps[d]
                totals[r + row_steps[d], col] += summed[m * 8 : m * 8 + 8]

    def group_of(r, g):
        forces(r, g, every)
        scatter(r, g)

    def step(state, sums, live):
        safe = jnp.where(live, state[9], 1.0)
        mass = density * safe * safe * safe
        inverse = 1.0 / mass
        spin_inverse = 1.0 / (0.4 * mass * safe * safe)
        new = [None] * components
        for c in range(3):
            accel = sums[c] * inverse
            if c == 2:
                accel = accel - gravity
            speed = state[3 + c] + timestep_length * accel
            new[c] = state[c] + timestep_length * speed
            new[3 + c] = speed
            new[6 + c] = state[6 + c] + timestep_length * sums[3 + c] * spin_inverse
        new[9] = state[9]
        new[10] = state[10] + timestep_length * sums[6] * inverse
        return [jnp.where(live, v, 0.0) for v in new]

    def step_group(r, g):
        cells = slice(g * TILE, (g + 1) * TILE)
        sums = [totals[r, 1 + g * TILE : 1 + (g + 1) * TILE, c, :] for c in range(7)]
        live = lane_f < filled_wide[r, cells, :]
        state = [ghost[c, r, TILE + g * TILE : 2 * TILE + g * TILE, :] for c in range(components)]
        for c, value in enumerate(step(state, sums, live)):
            out_ref[c, r, cells, :] = value

    def list_of(direction, r):
        cell_line = jnp.full((1, slots), -1, jnp.int32)
        slot_line = jnp.zeros((1, slots), jnp.int32)
        for k in range(movers):
            cell_line = jnp.where(line_lane == k, out_movers[direction, 0, 0, k] - r * cols, cell_line)
            slot_line = jnp.where(line_lane == k, out_movers[direction, 1, 0, k], slot_line)
        cell_line = jnp.where(line_lane < move_count[0, 0, direction], cell_line, -1)
        return cell_line, slot_line

    def chosen_of(cell_line, slot_line):
        chosen = cell_ids == cell_line
        slot_f = jnp.where(chosen, jnp.broadcast_to(slot_line + 1, (cols, slots)).astype(jnp.float32), 0.0)
        slot_of = jnp.sum(slot_f, axis=1, keepdims=True).astype(jnp.int32) - 1
        slot_of = jnp.broadcast_to(slot_of, (cols, slots))
        index = jnp.maximum(slot_of, 0)

        def line_of(value):
            return jnp.sum(jnp.where(chosen, lanes_of(value, index), 0.0), axis=0, keepdims=True)

        return line_of, lane_ids == slot_of

    def put(direction, r, there, message):
        key = jnp.zeros((1, slots), jnp.int32)
        cell_line = jnp.full((1, slots), -1, jnp.int32)
        for k in range(movers):
            hit = line_lane == in_movers[direction, 1, 0, k]
            key = jnp.where(hit, k, key)
            cell_line = jnp.where(hit, in_movers[direction, 0, 0, k] - r * cols, cell_line)
        cell_line = jnp.where(there, cell_line, -1)
        landing = cell_ids == cell_line
        key = jnp.broadcast_to(key, message.shape)
        values = lanes_of(message, key)
        for c in range(components):
            out_ref[c, r] = jnp.where(landing, values[c : c + 1], out_ref[c, r])

    lax.fori_loop(0, wide, clear, 0)
    msg_out[...] = jnp.zeros(msg_out.shape, jnp.float32)
    landed[...] = jnp.zeros(landed.shape, jnp.float32)
    own[0].wait()
    pack()
    pl.semaphore_wait(barrier, expected)
    start("side right", "side left", ("ghost", 0), "corner left", "corner right")
    start(*(("ghost", n) for n in range(1, groups)))
    for copy in own[1:]:
        copy.wait()
    for r in range(rows):
        spread(count_own, r, count_wide, r)
        spread(filled_ref, r, filled_wide, r)

    def inner(n, r):
        group_of(r, n)
        return r

    def outer(n, r):
        group_of(r, (groups - 1) * n)
        return r

    for r in range(rows - 1):
        lax.fori_loop(1, groups - 1, inner, r)
    arrive("side right", "side left")
    for r in range(rows - 1):
        lax.fori_loop(0, 2, outer, r)
    last = rows - 1
    forces(last, groups - 1, (2,))
    ahead = summed_of(last, groups - 1, TILE - 1, contacts_of(last, groups - 1), (2,), False)
    for r in range(rows):
        edge_out[0, r] = totals[r, 0]
        edge_out[1, r] = totals[r, wide - 1] + ahead if r == last else totals[r, wide - 1]
    start("edge low", "edge high")
    cells_back, slots_back = list_of(1, 0)
    lines_back, left_back = chosen_of(cells_back, slots_back)
    arrive("edge low", "edge high")
    for r in range(rows):
        totals[r, 1] += jnp.where(has[0, -1], owed_low[r], 0.0)
        totals[r, cols] += jnp.where(has[0, 1], owed_high[r], 0.0)
    for c in range(7):
        msg_out[1, c : c + 1, :] = lines_back(totals[0, 1 : 1 + cols, c, :])
    msg_out[1, 7:8, :] = cells_back.astype(jnp.float32)
    msg_out[1, 8:9, :] = slots_back.astype(jnp.float32)
    start("backward")
    for r in range(1, last):
        for g in range(groups):
            step_group(r, g)

    for g in range(groups):
        arrive(("ghost", g))
        if g == 0:
            unpack(0)
            unpack(1)
            arrive("corner left")
        elif g < groups - 1:
            unpack(g * TILE + 1)
        else:
            unpack(g * TILE)
            arrive("corner right")
        group_of(last, g)
        start(("owed", g))
        if g == 0:
            start("late high", "diag high")
        if g == groups - 1:
            start("late low", "diag low")
        step_group(last, g)
    cells_on, slots_on = list_of(0, last)
    lines_on, left_on = chosen_of(cells_on, slots_on)
    for c in range(components):
        value = out_ref[c, last]
        line = lines_on(value)
        if c == 0:
            line = line - jnp.where(cells_on >= 0, 1.0, 0.0)
        msg_out[0, c : c + 1, :] = line
        out_ref[c, last] = jnp.where(left_on, 0.0, value)
    start("forward")

    arrive("late low", "late high", "backward")
    message = jnp.where(has[1, 0], msg_in[1], 0.0)
    cells_new = message[7:8].astype(jnp.int32)
    lines_new, _ = chosen_of(cells_new, message[8:9].astype(jnp.int32))
    sums = []
    for c in range(7):
        value = totals[rows, 1 : 1 + cols, c, :]
        value = value + jnp.where((cell_ids == 0) & has[0, -1], late_low[c : c + 1, :], 0.0)
        value = value + jnp.where((cell_ids == cols - 1) & has[0, 1], late_high[c : c + 1, :], 0.0)
        sums.append(lines_new(value) + message[c : c + 1])
    state = [lines_new(ghost[c, rows, own_cols, :]) for c in range(components)]
    moving = cells_new >= 0
    for c, value in enumerate(step(state, sums, moving)):
        if c == 0:
            value = value + jnp.where(moving, 1.0, 0.0)
        landed[c : c + 1, :] = value
    put(1, last, has[1, 0], landed[...])

    arrive(("owed", 0), "diag low")
    totals[0, 1] += jnp.where(has[-1, -1], owed_diag[0], 0.0)
    for g in range(groups):
        if g + 1 < groups:
            arrive(("owed", g + 1))
        if g == groups - 1:
            arrive("diag high")
            totals[0, cols] += jnp.where(has[-1, 1], owed_diag[1], 0.0)
        cells = slice(g * TILE, (g + 1) * TILE)
        for n in range(g * TILE, (g + 1) * TILE):
            totals[0, 1 + n] += jnp.where(has[-1, 0], owed[n], 0.0)
        step_group(0, g)
    for c in range(components):
        out_ref[c, 0] = jnp.where(left_back, 0.0, out_ref[c, 0])
    arrive("forward")
    put(0, 0, has[-1, 0], msg_in[0])
    sent(*moves)


def body(blades, spans, particles, filled, contact_pairs, contact_count, movers_out, movers_in, move_count):
    components, rows, cols, slots = particles.shape
    padded = -(-components // 8) * 8
    f32, i32 = jnp.float32, jnp.int32
    riders = packing(components, slots, movers_out.shape[3])[3]
    remote_copies = 2 * (cols // TILE) + 12
    return pl.pallas_call(
        functools.partial(kernel, particles.shape, blades, spans),
        out_shape=pltpu.VMEM(particles.shape, f32),
        in_specs=[pl.BlockSpec(memory_space=pl.ANY)] * 7,
        out_specs=pl.BlockSpec(memory_space=pltpu.VMEM),
        scratch_shapes=[
            pltpu.VMEM((components, rows + 1, cols + 2 * TILE, slots), f32),
            pltpu.VMEM((components - riders, cols, slots), f32),
            pltpu.VMEM((2, rows, cols, contact_pairs.shape[3]), i32),
            pltpu.VMEM((rows, cols), i32),
            pltpu.VMEM((rows, cols), i32),
            pltpu.SMEM(movers_out.shape, i32),
            pltpu.SMEM(movers_in.shape, i32),
            pltpu.SMEM((1, 1, 2), i32),
            pltpu.VMEM((rows * cols * 8, slots), f32),
            pltpu.VMEM((rows * cols * 8, slots), f32),
            pltpu.VMEM((rows, cols, slots), f32),
            pltpu.VMEM((rows, cols, slots), f32),
            pltpu.VMEM((rows + 1, cols + 2, 8, slots), f32),
            pltpu.VMEM((2, rows, 8, slots), f32),
            pltpu.VMEM((rows, 8, slots), f32),
            pltpu.VMEM((rows, 8, slots), f32),
            pltpu.VMEM((8, slots), f32),
            pltpu.VMEM((8, slots), f32),
            pltpu.VMEM((cols, 8, slots), f32),
            pltpu.VMEM((2, 8, slots), f32),
            pltpu.VMEM((2, padded, slots), f32),
            pltpu.VMEM((2, padded, slots), f32),
            pltpu.VMEM((padded, slots), f32),
            pltpu.SemaphoreType.DMA((8,)),
            pltpu.SemaphoreType.DMA((remote_copies,)),
            pltpu.SemaphoreType.DMA((remote_copies,)),
        ],
        compiler_params=pltpu.CompilerParams(
            collective_id=0, has_side_effects=True, vmem_limit_bytes=VMEM_GRANT
        ),
    )(
        *(
            pltpu.with_memory_space_constraint(x, pltpu.HBM)
            for x in (
                particles,
                filled,
                contact_pairs,
                contact_count,
                movers_out,
                movers_in,
                jnp.transpose(move_count, (1, 2, 0)),
            )
        )
    )


def solution(mesh):
    sizes = dict(mesh.shape)
    return jax.shard_map(
        functools.partial(body, sizes["blade"], sizes["span"]),
        mesh=mesh,
        in_specs=(
            P(None, "blade", "span", None),
            P("blade", "span"),
            P(None, "blade", "span", None),
            P("blade", "span"),
            P(None, None, "blade", "span"),
            P(None, None, "blade", "span"),
            P(None, "blade", "span"),
        ),
        out_specs=P(None, "blade", "span", None),
        check_vma=False,
    )
```

time: 22.2 us -> 15 us (0.68)
  the two profiles are of different devices: /device:TPU:0 before, /device:TPU:17 now
where the time goes in v2:
time: 15 us; the launch traced here: 14.9 us
  Pallas kernels  14.1 us (94%)
  local copies, waits for them, and re-layouts  0.74 us (5%)
    pallas_call x1, Pallas kernels, body(): pl.pallas_call(functools.partial(kernel, particles.shape, blades, spans),...  14.1 us
    unnamed x1, local copies, waits for them, and re-layouts  0.74 us

profile of v2, /device:TPU:17, one launch (start us, length us, event | category | flops | bytes accessed | tf_op | source)
XLA Modules:
  0.0 14.9 jit_solution(3914804805220162864)
XLA Ops:
  0.0 14.1 %shard_map.73 = f32[11,2,32,128]{3,2,1,0:T(8,128)S(1)} custom-call(f32[11,2,32,128]{3,2,1,0:T(8,128)} %parts_hbm.1, s32[2,32]{1,0:T(2,128)} %filled_hbm.1, s32[2,2,32,128]{3,2,1,0:T(8,128)} %pairs_hbm.1, s32[2,32]{1,0:T(2,128)} %count_hbm.1, s32[2,2,1,16]{3,2,1,0:T(1,128)} %out_movers_hbm.1, s32[2,2,1,16]{3,2,1,0:T(1,128)} %in_movers_hbm.1, s32[1,1,2]{2,1,0:T(1,128)} %bitcast.1), custom_call_target="tpu_custom_call" | custom-call | tf_op jit(solution)/shard_map/pallas_call | solution.py:520
  14.1 0.7 %copy.9 = f32[11,2,32,128]{3,2,1,0:T(8,128)} copy(f32[11,2,32,128]{3,2,1,0:T(8,128)S(1)} %shard_map.73) | data formatting | bytes 720896

commit v3 on v2

v3 whole, which is shorter than its diff:
```python
import functools

import jax
import jax.numpy as jnp
from jax import lax
from jax.experimental import pallas as pl
from jax.experimental.pallas import tpu as pltpu
from jax.sharding import PartitionSpec as P

spring = 4.0
normal_damp = 0.5
tangent_damp = 0.3
conduct = 40.0
timestep_length = 0.05
density = 100.0
gravity = 9.81
soft_len = 0.05
row_steps = (0, 1, 0, 1, 1)
col_steps = (0, 0, 1, 1, -1)
MESH = pl.DeviceIdType.MESH
TILE = 8
VMEM_GRANT = 16 << 20


def cross(a, b):
    return (
        a[1] * b[2] - a[2] * b[1],
        a[2] * b[0] - a[0] * b[2],
        a[0] * b[1] - a[1] * b[0],
    )


def lanes_of(table, index):
    return jnp.take_along_axis(table, index, axis=1, mode="promise_in_bounds")


def pair_terms(first, second, row_shift, col_shift, live):
    gap = (
        second[0] + row_shift - first[0],
        second[1] + col_shift - first[1],
        second[2] - first[2],
    )
    distance = jnp.sqrt(gap[0] * gap[0] + gap[1] * gap[1] + gap[2] * gap[2] + soft_len * soft_len)
    inverse = 1.0 / distance
    normal = tuple(g * inverse for g in gap)
    rad_first, rad_second = first[9], second[9]
    intersection = rad_first + rad_second - distance
    spin = tuple(rad_first * first[6 + c] + rad_second * second[6 + c] for c in range(3))
    turn = cross(spin, normal)
    relative = tuple(second[3 + c] - first[3 + c] - turn[c] for c in range(3))
    speed = relative[0] * normal[0] + relative[1] * normal[1] + relative[2] * normal[2]
    friction = tuple(tangent_damp * (relative[c] - speed * normal[c]) for c in range(3))
    push = normal_damp * speed - spring * intersection
    force = tuple(push * normal[c] + friction[c] for c in range(3))
    torque = cross(normal, friction)
    denom = jnp.where(live, rad_first + rad_second, 1.0)
    heat = 2.0 * conduct * rad_first * rad_second / denom * (second[10] - first[10])
    on_first = force + tuple(rad_first * t for t in torque) + (heat,)
    on_second = tuple(-f for f in force) + tuple(rad_second * t for t in torque) + (-heat,)
    keep = lambda v: jnp.where(live, v, 0.0)
    return [keep(v) for v in on_first], [keep(v) for v in on_second]


def order_of(cols):
    groups = cols // TILE
    return [0, groups - 1, *range(1, groups - 1)]


def ghost_chunk(g, cols):
    groups = cols // TILE
    if g == 0:
        return 0, TILE + 1
    if g == groups - 1:
        return cols - TILE - 1, cols
    return g * TILE + 1, min((g + 1) * TILE + 1, cols - TILE - 1)


def owed_chunk(g, cols):
    groups = cols // TILE
    if g == 0:
        return 0, TILE - 1
    if g == groups - 1:
        return cols - TILE + 1, cols
    return g * TILE - 1, ((g + 1) * TILE - 1 if g < groups - 2 else cols - TILE + 1)


def packing(components, slots, movers):
    live = slots - 2 * movers
    spare = slots - live
    pieces = live // spare
    riders = components // (pieces + 1) if live % spare == 0 else 0
    return live, spare, pieces, riders


def far_boundaries(mesh):
    line = mesh.devices.reshape(mesh.devices.shape[0], -1)[:, 0]
    hops = [
        sum(abs(p - q) for p, q in zip(a.coords, b.coords)) for a, b in zip(line, line[1:])
    ]
    most = max(hops, default=0)
    if most == min(hops, default=0):
        return ()
    return tuple(n for n, h in enumerate(hops) if h >= most)


def is_far(boundary, blades, fars):
    for period in range(1, blades):
        if fars == tuple(range(period - 1, blades - 1, period)):
            return lax.rem(boundary + period, period) == period - 1
    far = boundary < -1
    for f in fars:
        far = far | (boundary == f)
    return far


def kernel(
    shape,
    blades,
    spans,
    fars,
    parts_hbm,
    filled_hbm,
    pairs_hbm,
    count_hbm,
    out_movers_hbm,
    in_movers_hbm,
    move_count_hbm,
    out_ref,
    ghost,
    packed,
    packed_last,
    pairs_ref,
    count_own,
    count_prev,
    filled_ref,
    out_movers,
    in_movers,
    move_count,
    first_terms,
    second_terms,
    count_wide,
    filled_wide,
    totals,
    edge_out,
    owed_low,
    owed_high,
    late_low,
    late_high,
    seam_out,
    seam_in,
    owed,
    owed_diag,
    msg_out,
    msg_in,
    landed,
    local_sem,
    send_sem,
    recv_sem,
):
    components, rows, cols, slots = shape
    movers = out_movers.shape[3]
    wide = cols + 2
    groups = cols // TILE
    live_slots, spare, pieces, riders = packing(components, slots, movers)
    carried = components - riders
    order = order_of(cols)
    middle = order[2:]
    seams = (TILE - 1, TILE, cols - TILE - 1, cols - TILE)
    i = lax.axis_index("blade")
    j = lax.axis_index("span")
    has = {}
    for di in (-1, 0, 1):
        for dj in (-1, 0, 1):
            if (di, dj) != (0, 0):
                a, b = i + di, j + dj
                has[di, dj] = (a >= 0) & (a < blades) & (b >= 0) & (b < spans)
    far_up = has[1, 0] & is_far(i, blades, fars)
    far_down = has[-1, 0] & is_far(i - 1, blades, fars)
    before = rows + 1

    own_cols = slice(TILE, TILE + cols)
    own = [
        pltpu.make_async_copy(source, target, local_sem.at[n])
        for n, (source, target) in enumerate(
            (
                (parts_hbm.at[:, 0], ghost.at[:, 0, own_cols, :]),
                (count_hbm, count_own),
                (filled_hbm, filled_ref),
                (pairs_hbm, pairs_ref.at[:, 0:rows]),
                (parts_hbm.at[:, 1:rows], ghost.at[:, 1:rows, own_cols, :]),
                (out_movers_hbm, out_movers),
                (in_movers_hbm, in_movers),
                (move_count_hbm, move_count),
            )
        )
    ]
    barrier = pltpu.get_barrier_semaphore()
    expected = jnp.int32(0)
    for (di, dj), there in has.items():
        expected = expected + there.astype(jnp.int32)

        @pl.when(there)
        def _(di=di, dj=dj):
            pl.semaphore_signal(
                barrier, inc=1, device_id=(i + di, j + dj), device_id_type=MESH
            )

    for copy in own:
        copy.start()

    moves = {}

    def move(name, source, target, di, dj, far=None):
        n = len(moves)
        copy = pltpu.make_async_remote_copy(
            src_ref=source,
            dst_ref=target,
            send_sem=send_sem.at[n],
            recv_sem=recv_sem.at[n],
            device_id=(i + di, j + dj),
            device_id_type=MESH,
        )
        sends, comes = has[di, dj], has[-di, -dj]
        if far is not None:
            sends = sends & (far_up if far else ~far_up)
            comes = comes & (far_down if far else ~far_down)
        moves[name] = (copy, sends, comes)

    low = slice(0, 1)
    high = slice(cols - 1, cols)
    left = slice(TILE - 1, TILE)
    right = slice(TILE + cols, TILE + cols + 1)
    for g in order:
        a, b = ghost_chunk(g, cols)
        target = ghost.at[0:carried, rows, TILE + a : TILE + b, :]
        move(("ghost", g), packed.at[:, a:b], target, -1, 0)
    move("corner right", parts_hbm.at[:, 0, low, :], ghost.at[:, rows, right, :], -1, -1)
    move("corner left", parts_hbm.at[:, 0, high, :], ghost.at[:, rows, left, :], -1, 1)
    move("side right", parts_hbm.at[:, :, low, :], ghost.at[:, 0:rows, right, :], 0, -1)
    move("side left", parts_hbm.at[:, :, high, :], ghost.at[:, 0:rows, left, :], 0, 1)
    move("edge low", edge_out.at[1], owed_low, 0, 1)
    move("edge high", edge_out.at[0], owed_high, 0, -1)
    move("late low", totals.at[rows, wide - 1], late_low, 0, 1)
    move("late high", totals.at[rows, 0], late_high, 0, -1)
    for g in order:
        a, b = owed_chunk(g, cols)
        mode = False if g in middle else None
        move(("owed", g), totals.at[rows, 1 + a : 1 + b], owed.at[a:b], 1, 0, mode)
    move("diag low", totals.at[rows, wide - 1], owed_diag.at[0], 1, 1)
    move("diag high", totals.at[rows, 0], owed_diag.at[1], 1, -1)
    move("seams", seam_out, seam_in, 1, 0, True)
    inner_cols = slice(TILE, cols - TILE)
    target = pairs_ref.at[:, rows, inner_cols]
    move("far pairs", pairs_hbm.at[:, rows - 1, inner_cols], target, 1, 0, True)
    move("far count", count_hbm, count_prev, 1, 0, True)
    for g in middle:
        a, b = g * TILE, (g + 1) * TILE
        target = ghost.at[0:carried, before, TILE + a : TILE + b, :]
        move(("far", g), packed_last.at[:, a:b], target, 1, 0, True)
    move("forward", msg_out.at[0], msg_in.at[0], 1, 0)
    move("backward", msg_out.at[1], msg_in.at[1], -1, 0)

    def start(*which):
        for w in which:
            copy, sends, comes = moves[w]

            @pl.when(sends)
            def _(copy=copy):
                copy.start()

    def arrive(*which):
        for w in which:
            copy, sends, comes = moves[w]

            @pl.when(comes)
            def _(copy=copy):
                copy.wait_recv()

    def sent(*which):
        for w in which:
            copy, sends, comes = moves[w]

            @pl.when(sends)
            def _(copy=copy):
                copy.wait_send()

    diagonal = lax.broadcasted_iota(jnp.int32, (cols, cols), 0) == lax.broadcasted_iota(
        jnp.int32, (cols, cols), 1
    )
    lane = lax.broadcasted_iota(jnp.int32, (TILE, slots), 1)
    lane_f = lane.astype(jnp.float32)
    slot_ids = lax.broadcasted_iota(jnp.int32, (slots, slots), 0)
    line_lane = lax.broadcasted_iota(jnp.int32, (1, slots), 1)
    cell_ids = lax.broadcasted_iota(jnp.int32, (cols, slots), 0)
    lane_ids = lax.broadcasted_iota(jnp.int32, (cols, slots), 1)

    def spread(source, r, target, at):
        line = jnp.broadcast_to(source[r : r + 1, :].astype(jnp.float32), (cols, cols))
        column = jnp.sum(jnp.where(diagonal, line, 0.0), axis=1, keepdims=True)
        target[at] = jnp.broadcast_to(column, (cols, slots))

    def clear(n, _):
        for r in range(rows + 2):
            totals[r, n] = jnp.zeros((8, slots), jnp.float32)
        return 0

    def pack(r, target):
        for c in range(carried):
            value = ghost[c, r, own_cols, :]
            if c < riders * pieces:
                rider, piece = carried + c // pieces, c % pieces
                shift = live_slots - piece * spare
                moved = pltpu.roll(ghost[rider, r, own_cols, :], shift, 1)
                value = jnp.where(lane_ids < live_slots, value, moved)
            target[c] = value

    def unpack(r, at):
        for e in range(riders):
            value = None
            for piece in range(pieces):
                shift = (piece * spare - live_slots) % slots
                tile = ghost[e * pieces + piece, r, TILE + at : 2 * TILE + at, :]
                moved = pltpu.roll(tile, shift, 1)
                value = moved if piece == 0 else jnp.where(lane >= piece * spare, moved, value)
            ghost[carried + e, r, TILE + at : 2 * TILE + at, :] = value

    def tiles_of(g):
        return g * TILE if isinstance(g, int) else pl.multiple_of(g * TILE, TILE)

    def row_of(r):
        if r == before:
            return before, rows, lambda d: 0
        return r, r, lambda d: r + row_steps[d]

    def contacts_of(r, g):
        at = tiles_of(g)
        _, listed, _ = row_of(r)
        ids = pairs_ref[0, listed, pl.ds(at, TILE), :]
        code = pairs_ref[1, listed, pl.ds(at, TILE), :]
        heading = code // slots
        return ids, heading, code - heading * slots

    def forces(r, g, headings):
        at = tiles_of(g)
        near, listed, far_row = row_of(r)
        ids, heading, target = contacts_of(r, g)
        live = lane_f < count_wide[listed, pl.ds(at, TILE), :]
        if len(headings) < len(row_steps):
            among = heading == headings[0]
            for d in headings[1:]:
                among = among | (heading == d)
            live = live & among
        first = [
            lanes_of(ghost[c, near, pl.ds(at + TILE, TILE), :], ids) for c in range(components)
        ]
        second = [None] * components
        for n, d in enumerate(headings):
            pick = heading == d
            for c in range(components):
                rows_at = pl.ds(at + TILE + col_steps[d], TILE)
                value = lanes_of(ghost[c, far_row(d), rows_at, :], target)
                second[c] = value if n == 0 else jnp.where(pick, value, second[c])
        row_shift = jnp.where((heading == 0) | (heading == 2), 0.0, 1.0)
        col_shift = jnp.where(
            (heading == 2) | (heading == 3), 1.0, jnp.where(heading == 4, -1.0, 0.0)
        )
        on_first, on_second = pair_terms(first, second, row_shift, col_shift, live)
        zero = jnp.zeros((TILE, slots), jnp.float32)
        base = (listed * cols + g * TILE) * 8
        for c, (a, b) in enumerate(zip(on_first + [zero], on_second + [zero])):
            first_terms[pl.ds(base + c, TILE, stride=8), :] = a
            second_terms[pl.ds(base + c, TILE, stride=8), :] = b

    def scatter(r, g, headings):
        near, listed, far_row = row_of(r)
        ids, heading, target = contacts_of(r, g)
        shared = 0 in headings
        zero = jnp.zeros((8, slots), jnp.float32)
        for n in range(TILE):
            base = (listed * cols + g * TILE + n) * 8
            if not isinstance(base, int):
                base = pl.multiple_of(base, 8)
            a = first_terms[pl.ds(base, 8), :]
            b = second_terms[pl.ds(base, 8), :]
            head = heading[n : n + 1]
            blocks = [jnp.where(head == d, b, 0.0) for d in headings]
            if not shared:
                blocks = [zero] + blocks
            near_blocks = [a] + [zero] * (len(blocks) - 1)
            terms = jnp.concatenate(
                [jnp.concatenate(near_blocks, axis=0), jnp.concatenate(blocks, axis=0)], axis=1
            )
            near_hot = jnp.where(slot_ids == ids[n : n + 1], 1.0, 0.0)
            hot = jnp.where(slot_ids == target[n : n + 1], 1.0, 0.0)
            hot = jnp.concatenate([near_hot, hot], axis=1)
            coarse = terms.astype(jnp.bfloat16).astype(jnp.float32)
            split = jnp.concatenate([coarse, terms - coarse], axis=0).astype(jnp.bfloat16)
            summed = lax.dot_general(
                split,
                hot.astype(jnp.bfloat16),
                (((1,), (1,)), ((), ())),
                preferred_element_type=jnp.float32,
            )
            count = len(blocks) * 8
            summed = summed[:count] + summed[count:]
            places = [(far_row(d), col_steps[d]) for d in headings]
            if not shared:
                places = [(near, 0)] + places
            for m, (row, shift) in enumerate(places):
                totals[row, g * TILE + n + 1 + shift] += summed[m * 8 : m * 8 + 8]

    every, inside, across = (0, 1, 2, 3, 4), (0, 2), (1, 3, 4)

    def group_of(r, g, headings):
        forces(r, g, headings)
        scatter(r, g, headings)

    def step(state, sums, live):
        safe = jnp.where(live, state[9], 1.0)
        mass = density * safe * safe * safe
        inverse = 1.0 / mass
        spin_inverse = 1.0 / (0.4 * mass * safe * safe)
        new = [None] * components
        for c in range(3):
            accel = sums[c] * inverse
            if c == 2:
                accel = accel - gravity
            speed = state[3 + c] + timestep_length * accel
            new[c] = state[c] + timestep_length * speed
            new[3 + c] = speed
            new[6 + c] = state[6 + c] + timestep_length * sums[3 + c] * spin_inverse
        new[9] = state[9]
        new[10] = state[10] + timestep_length * sums[6] * inverse
        return [jnp.where(live, v, 0.0) for v in new]

    def step_group(r, g, left=None):
        cells = slice(g * TILE, (g + 1) * TILE)
        sums = [totals[r, 1 + g * TILE : 1 + (g + 1) * TILE, c, :] for c in range(7)]
        live = lane_f < filled_wide[r, cells, :]
        state = [ghost[c, r, TILE + g * TILE : 2 * TILE + g * TILE, :] for c in range(components)]
        if left is not None:
            live = live & ~left[cells]
        for c, value in enumerate(step(state, sums, live)):
            out_ref[c, r, cells, :] = value

    def list_of(direction, r):
        cell_line = jnp.full((1, slots), -1, jnp.int32)
        slot_line = jnp.zeros((1, slots), jnp.int32)
        for k in range(movers):
            cell_line = jnp.where(line_lane == k, out_movers[direction, 0, 0, k] - r * cols, cell_line)
            slot_line = jnp.where(line_lane == k, out_movers[direction, 1, 0, k], slot_line)
        cell_line = jnp.where(line_lane < move_count[0, 0, direction], cell_line, -1)
        return cell_line, slot_line

    def chosen_of(cell_line, slot_line):
        chosen = cell_ids == cell_line
        slot_f = jnp.where(chosen, jnp.broadcast_to(slot_line + 1, (cols, slots)).astype(jnp.float32), 0.0)
        slot_of = jnp.sum(slot_f, axis=1, keepdims=True).astype(jnp.int32) - 1
        slot_of = jnp.broadcast_to(slot_of, (cols, slots))
        index = jnp.maximum(slot_of, 0)

        def line_of(value):
            return jnp.sum(jnp.where(chosen, lanes_of(value, index), 0.0), axis=0, keepdims=True)

        return line_of, lane_ids == slot_of

    def put(direction, r, there, message):
        key = jnp.zeros((1, slots), jnp.int32)
        cell_line = jnp.full((1, slots), -1, jnp.int32)
        for k in range(movers):
            hit = line_lane == in_movers[direction, 1, 0, k]
            key = jnp.where(hit, k, key)
            cell_line = jnp.where(hit, in_movers[direction, 0, 0, k] - r * cols, cell_line)
        cell_line = jnp.where(there, cell_line, -1)
        landing = cell_ids == cell_line
        key = jnp.broadcast_to(key, message.shape)
        values = lanes_of(message, key)
        for c in range(components):
            out_ref[c, r] = jnp.where(landing, values[c : c + 1], out_ref[c, r])

    def finish(direction, message, row, extra, state_of):
        cells_new = message[7:8].astype(jnp.int32)
        lines_new, _ = chosen_of(cells_new, message[8:9].astype(jnp.int32))
        sums = [
            lines_new(extra(c, totals[row, 1 : 1 + cols, c, :])) + message[c : c + 1]
            for c in range(7)
        ]
        state = [state_of(c, lines_new) for c in range(components)]
        moving = cells_new >= 0
        for c, value in enumerate(step(state, sums, moving)):
            if c == 0:
                value = value + jnp.where(moving, -1.0 if direction == 0 else 1.0, 0.0)
            landed[direction, c : c + 1, :] = value

    def share_of(direction, r, lines, cells_line, slots_line):
        for c in range(7):
            msg_out[direction, c : c + 1, :] = lines(totals[r, 1 : 1 + cols, c, :])
        msg_out[direction, 7:8, :] = cells_line.astype(jnp.float32)
        msg_out[direction, 8:9, :] = slots_line.astype(jnp.float32)

    last = rows - 1
    lax.fori_loop(0, wide, clear, 0)
    msg_out[...] = jnp.zeros(msg_out.shape, jnp.float32)
    landed[...] = jnp.zeros(landed.shape, jnp.float32)
    own[0].wait()
    pack(0, packed)
    own[4].wait()

    @pl.when(far_up)
    def _():
        pack(last, packed_last)

    pl.semaphore_wait(barrier, expected)
    start("side right", "side left", ("ghost", 0), "corner left", "corner right")
    start(*(("ghost", g) for g in order[1:]))
    for n, copy in enumerate(own):
        if n not in (0, 4):
            copy.wait()
    for r in range(rows):
        spread(count_own, r, count_wide, r)
        spread(filled_ref, r, filled_wide, r)

    def early(g):
        for r in range(last):
            group_of(r, g, every)
        group_of(last, g, inside)

    def inner(n, _):
        early(n)
        return 0

    def outer(n, _):
        early((groups - 1) * n)
        return 0

    lax.fori_loop(1, groups - 1, inner, 0)
    arrive("side right", "side left")
    lax.fori_loop(0, 2, outer, 0)
    for r in range(rows):
        edge_out[0, r] = totals[r, 0]
        edge_out[1, r] = totals[r, wide - 1]
    start("edge low", "edge high")
    cells_back, slots_back = list_of(1, 0)
    lines_back, left_back = chosen_of(cells_back, slots_back)
    cells_on, slots_on = list_of(0, last)
    lines_on, left_on = chosen_of(cells_on, slots_on)
    arrive("edge low", "edge high")
    for r in range(rows):
        totals[r, 1] += jnp.where(has[0, -1], owed_low[r], 0.0)
        totals[r, cols] += jnp.where(has[0, 1], owed_high[r], 0.0)
    share_of(1, 0, lines_back, cells_back, slots_back)
    start("backward")
    start("far pairs", "far count", *(("far", g) for g in middle))

    for r in range(1, last):
        for g in range(groups):
            step_group(r, g)

    def last_group(g):
        arrive(("ghost", g))
        if g == 0:
            unpack(rows, 0)
            unpack(rows, 1)
            arrive("corner left")
        elif g == groups - 1:
            unpack(rows, cols - TILE - 1)
            unpack(rows, cols - TILE)
            arrive("corner right")
        else:
            unpack(rows, g * TILE + 1)
        group_of(last, g, across)
        start(("owed", g))

    last_group(0)
    start("late high", "diag high")
    last_group(groups - 1)
    start("late low", "diag low")

    @pl.when(far_up)
    def _():
        for n, col in enumerate(seams):
            seam_out[n] = totals[rows, 1 + col]
        start("seams")
        share_of(0, last, lines_on, cells_on, slots_on)
        for c in range(components):
            msg_out[0, 9 + c : 10 + c, :] = lines_on(ghost[c, last, own_cols, :])
        start("forward")

    for g in middle:
        last_group(g)
    for g in range(groups):
        step_group(last, g)

    @pl.when(has[1, 0] & ~far_up)
    def _():
        for c in range(components):
            line = lines_on(out_ref[c, last])
            if c == 0:
                line = line - jnp.where(cells_on >= 0, 1.0, 0.0)
            msg_out[0, c : c + 1, :] = line
        start("forward")

    for c in range(components):
        out_ref[c, last] = jnp.where(left_on, 0.0, out_ref[c, last])

    def late_edges(c, value):
        value = value + jnp.where((cell_ids == 0) & has[0, -1], late_low[c : c + 1, :], 0.0)
        return value + jnp.where((cell_ids == cols - 1) & has[0, 1], late_high[c : c + 1, :], 0.0)

    arrive("late low", "late high", "backward")

    @pl.when(has[1, 0])
    def _():
        finish(1, msg_in[1], rows, late_edges, lambda c, lines: lines(ghost[c, rows, own_cols, :]))
        put(1, last, True, landed[1])

    def add_diagonals():
        totals[0, 1] += jnp.where(has[-1, -1], owed_diag[0], 0.0)
        totals[0, cols] += jnp.where(has[-1, 1], owed_diag[1], 0.0)

    @pl.when(far_down)
    def _():
        arrive("far count", "far pairs")
        spread(count_prev, last, count_wide, rows)
        for g in middle:
            arrive(("far", g))
            unpack(before, g * TILE)
            group_of(before, g, across)
        arrive(("owed", 0), ("owed", groups - 1), "seams", "diag low", "diag high")
        add_diagonals()
        for g in (0, groups - 1):
            for n in range(*owed_chunk(g, cols)):
                totals[0, 1 + n] += owed[n]
        for n, col in enumerate(seams):
            totals[0, 1 + col] += seam_in[n]
        for g in range(groups):
            step_group(0, g, left_back)
        arrive("forward")
        message = msg_in[0]
        finish(0, message, before, lambda c, value: value, lambda c, _: message[9 + c : 10 + c])

    @pl.when(~far_down)
    def _():
        arrive(("owed", 0), ("owed", groups - 1), "diag low", "diag high")
        add_diagonals()
        for k, g in enumerate(order):
            if k > 1:
                arrive(("owed", g))
            for n in range(*owed_chunk(g, cols)):
                totals[0, 1 + n] += jnp.where(has[-1, 0], owed[n], 0.0)
            if k > 1:
                step_group(0, g - 1, left_back)
        step_group(0, groups - 2, left_back)
        step_group(0, groups - 1, left_back)
        arrive("forward")
        landed[0, 0:components, :] = msg_in[0, 0:components, :]

    put(0, 0, has[-1, 0], landed[0])
    sent(*moves)


def body(blades, spans, fars, particles, filled, contact_pairs, contact_count, movers_out, movers_in, move_count):
    components, rows, cols, slots = particles.shape
    padded = -(-components // 8) * 8
    message = -(-(components + 9) // 8) * 8
    f32, i32 = jnp.float32, jnp.int32
    riders = packing(components, slots, movers_out.shape[3])[3]
    remote_copies = 3 * (cols // TILE) + 13
    return pl.pallas_call(
        functools.partial(kernel, particles.shape, blades, spans, fars),
        out_shape=pltpu.VMEM(particles.shape, f32),
        in_specs=[pl.BlockSpec(memory_space=pl.ANY)] * 7,
        out_specs=pl.BlockSpec(memory_space=pltpu.VMEM),
        scratch_shapes=[
            pltpu.VMEM((components, rows + 2, cols + 2 * TILE, slots), f32),
            pltpu.VMEM((components - riders, cols, slots), f32),
            pltpu.VMEM((components - riders, cols, slots), f32),
            pltpu.VMEM((2, rows + 1, cols, contact_pairs.shape[3]), i32),
            pltpu.VMEM((rows, cols), i32),
            pltpu.VMEM((rows, cols), i32),
            pltpu.VMEM((rows, cols), i32),
            pltpu.SMEM(movers_out.shape, i32),
            pltpu.SMEM(movers_in.shape, i32),
            pltpu.SMEM((1, 1, 2), i32),
            pltpu.VMEM(((rows + 1) * cols * 8, slots), f32),
            pltpu.VMEM(((rows + 1) * cols * 8, slots), f32),
            pltpu.VMEM((rows + 1, cols, slots), f32),
            pltpu.VMEM((rows, cols, slots), f32),
            pltpu.VMEM((rows + 2, cols + 2, 8, slots), f32),
            pltpu.VMEM((2, rows, 8, slots), f32),
            pltpu.VMEM((rows, 8, slots), f32),
            pltpu.VMEM((rows, 8, slots), f32),
            pltpu.VMEM((8, slots), f32),
            pltpu.VMEM((8, slots), f32),
            pltpu.VMEM((4, 8, slots), f32),
            pltpu.VMEM((4, 8, slots), f32),
            pltpu.VMEM((cols, 8, slots), f32),
            pltpu.VMEM((2, 8, slots), f32),
            pltpu.VMEM((2, message, slots), f32),
            pltpu.VMEM((2, message, slots), f32),
            pltpu.VMEM((2, padded, slots), f32),
            pltpu.SemaphoreType.DMA((8,)),
            pltpu.SemaphoreType.DMA((remote_copies,)),
            pltpu.SemaphoreType.DMA((remote_copies,)),
        ],
        compiler_params=pltpu.CompilerParams(
            collective_id=0, has_side_effects=True, vmem_limit_bytes=VMEM_GRANT
        ),
    )(
        *(
            pltpu.with_memory_space_constraint(x, pltpu.HBM)
            for x in (
                particles,
                filled,
                contact_pairs,
                contact_count,
                movers_out,
                movers_in,
                jnp.transpose(move_count, (1, 2, 0)),
            )
        )
    )


def solution(mesh):
    sizes = dict(mesh.shape)
    return jax.shard_map(
        functools.partial(body, sizes["blade"], sizes["span"], far_boundaries(mesh)),
        mesh=mesh,
        in_specs=(
            P(None, "blade", "span", None),
            P("blade", "span"),
            P(None, "blade", "span", None),
            P("blade", "span"),
            P(None, None, "blade", "span"),
            P(None, None, "blade", "span"),
            P(None, "blade", "span"),
        ),
        out_specs=P(None, "blade", "span", None),
        check_vma=False,
    )
```

time: 15 us -> 14.7 us (0.980)
  Pallas kernels: 14.1 us -> 13.7 us
    pallas_call x1, Pallas kernels: 14.1 us -> 13.7 us  [body(): pl.pallas_call(functools.partial(kernel, particles.shape, blades, spans,...]
where the time goes in v3:
time: 14.7 us; the launch traced here: 14.5 us
  Pallas kernels  13.7 us (93%)
  local copies, waits for them, and re-layouts  0.74 us (5%)
    pallas_call x1, Pallas kernels, body(): pl.pallas_call(functools.partial(kernel, particles.shape, blades, spans,...  13.7 us
    unnamed x1, local copies, waits for them, and re-layouts  0.74 us

profile of v3, /device:TPU:17, one launch (start us, length us, event | category | flops | bytes accessed | tf_op | source)
XLA Modules:
  0.0 14.5 jit_solution(6797480157828776049)
XLA Ops:
  0.0 13.7 %shard_map.73 = f32[11,2,32,128]{3,2,1,0:T(8,128)S(1)} custom-call(f32[11,2,32,128]{3,2,1,0:T(8,128)} %parts_hbm.1, s32[2,32]{1,0:T(2,128)} %filled_hbm.1, s32[2,2,32,128]{3,2,1,0:T(8,128)} %pairs_hbm.1, s32[2,32]{1,0:T(2,128)} %count_hbm.1, s32[2,2,1,16]{3,2,1,0:T(1,128)} %out_movers_hbm.1, s32[2,2,1,16]{3,2,1,0:T(1,128)} %in_movers_hbm.1, s32[1,1,2]{2,1,0:T(1,128)} %bitcast.1), custom_call_target="tpu_custom_call" | custom-call | tf_op jit(solution)/shard_map/pallas_call | solution.py:669
  13.7 0.7 %copy.9 = f32[11,2,32,128]{3,2,1,0:T(8,128)} copy(f32[11,2,32,128]{3,2,1,0:T(8,128)S(1)} %shard_map.73) | data formatting | bytes 720896

commit v4 on v3

--- a/solution.py
+++ b/solution.py
@@ -89,7 +89,8 @@
     spare = slots - live
     pieces = live // spare
     riders = components // (pieces + 1) if live % spare == 0 else 0
-    return live, spare, pieces, riders
+    sent_rows = 6 if live % spare == 0 and pieces <= 6 else 8
+    return live, spare, pieces, riders, sent_rows
 
 
 def far_boundaries(mesh):
@@ -161,7 +162,7 @@
     movers = out_movers.shape[3]
     wide = cols + 2
     groups = cols // TILE
-    live_slots, spare, pieces, riders = packing(components, slots, movers)
+    live_slots, spare, pieces, riders, sent_rows = packing(components, slots, movers)
     carried = components - riders
     order = order_of(cols)
     middle = order[2:]
@@ -245,7 +246,8 @@
     for g in order:
         a, b = owed_chunk(g, cols)
         mode = False if g in middle else None
-        move(("owed", g), totals.at[rows, 1 + a : 1 + b], owed.at[a:b], 1, 0, mode)
+        source, target = totals.at[rows, 1 + a : 1 + b, 0:sent_rows], owed.at[a:b, 0:sent_rows]
+        move(("owed", g), source, target, 1, 0, mode)
     move("diag low", totals.at[rows, wide - 1], owed_diag.at[0], 1, 1)
     move("diag high", totals.at[rows, 0], owed_diag.at[1], 1, -1)
     move("seams", seam_out, seam_in, 1, 0, True)
@@ -323,6 +325,28 @@
                 moved = pltpu.roll(tile, shift, 1)
                 value = moved if piece == 0 else jnp.where(lane >= piece * spare, moved, value)
             ghost[carried + e, r, TILE + at : 2 * TILE + at, :] = value
+
+    def load_heat(g):
+        if sent_rows == 8:
+            return
+        a, b = owed_chunk(g, cols)
+        for first in {a, b - TILE} if b - a >= TILE else {a}:
+            n = min(TILE, b - a)
+            cells = slice(1 + first, 1 + first + n)
+            heat = totals[rows, cells, 6, :]
+            spot = lax.broadcasted_iota(jnp.int32, (n, slots), 1) < live_slots
+            for piece in range(pieces):
+                moved = pltpu.roll(heat, live_slots - piece * spare, 1)
+                totals[rows, cells, piece, :] = jnp.where(spot, totals[rows, cells, piece, :], moved)
+
+    def owed_sum(c, cells):
+        if c < 6 or sent_rows == 8:
+            return owed[cells, c, :]
+        value = None
+        for piece in range(pieces):
+            moved = pltpu.roll(owed[cells, piece, :], (piece * spare - live_slots) % slots, 1)
+            value = moved if piece == 0 else jnp.where(lane >= piece * spare, moved, value)
+        return value
 
     def tiles_of(g):
         return g * TILE if isinstance(g, int) else pl.multiple_of(g * TILE, TILE)
@@ -436,6 +460,10 @@
     def step_group(r, g, left=None):
         cells = slice(g * TILE, (g + 1) * TILE)
         sums = [totals[r, 1 + g * TILE : 1 + (g + 1) * TILE, c, :] for c in range(7)]
+        if r == 0:
+            sums = [
+                v + jnp.where(has[-1, 0], owed_sum(c, cells), 0.0) for c, v in enumerate(sums)
+            ]
         live = lane_f < filled_wide[r, cells, :]
         state = [ghost[c, r, TILE + g * TILE : 2 * TILE + g * TILE, :] for c in range(components)]
         if left is not None:
@@ -464,17 +492,19 @@
 
         return line_of, lane_ids == slot_of
 
-    def put(direction, r, there, message):
+    def landing_of(direction, r):
         key = jnp.zeros((1, slots), jnp.int32)
         cell_line = jnp.full((1, slots), -1, jnp.int32)
         for k in range(movers):
             hit = line_lane == in_movers[direction, 1, 0, k]
             key = jnp.where(hit, k, key)
             cell_line = jnp.where(hit, in_movers[direction, 0, 0, k] - r * cols, cell_line)
-        cell_line = jnp.where(there, cell_line, -1)
-        landing = cell_ids == cell_line
-        key = jnp.broadcast_to(key, message.shape)
-        values = lanes_of(message, key)
+        return key, cell_line
+
+    def put(r, there, message, lists):
+        key, cell_line = lists
+        landing = cell_ids == jnp.where(there, cell_line, -1)
+        values = lanes_of(message, jnp.broadcast_to(key, message.shape))
         for c in range(components):
             out_ref[c, r] = jnp.where(landing, values[c : c + 1], out_ref[c, r])
 
@@ -513,6 +543,7 @@
     pl.semaphore_wait(barrier, expected)
     start("side right", "side left", ("ghost", 0), "corner left", "corner right")
     start(*(("ghost", g) for g in order[1:]))
+    start("far pairs", "far count")
     for n, copy in enumerate(own):
         if n not in (0, 4):
             copy.wait()
@@ -550,7 +581,8 @@
         totals[r, cols] += jnp.where(has[0, 1], owed_high[r], 0.0)
     share_of(1, 0, lines_back, cells_back, slots_back)
     start("backward")
-    start("far pairs", "far count", *(("far", g) for g in middle))
+    start(*(("far", g) for g in middle))
+    lists_first, lists_last = landing_of(0, 0), landing_of(1, last)
 
     for r in range(1, last):
         for g in range(groups):
@@ -569,6 +601,7 @@
         else:
             unpack(rows, g * TILE + 1)
         group_of(last, g, across)
+        load_heat(g)
         start(("owed", g))
 
     last_group(0)
@@ -612,7 +645,9 @@
     @pl.when(has[1, 0])
     def _():
         finish(1, msg_in[1], rows, late_edges, lambda c, lines: lines(ghost[c, rows, own_cols, :]))
-        put(1, last, True, landed[1])
+        put(last, has[1, 0], landed[1], lists_last)
+
+    sent(*moves)
 
     def add_diagonals():
         totals[0, 1] += jnp.where(has[-1, -1], owed_diag[0], 0.0)
@@ -628,9 +663,8 @@
             group_of(before, g, across)
         arrive(("owed", 0), ("owed", groups - 1), "seams", "diag low", "diag high")
         add_diagonals()
-        for g in (0, groups - 1):
-            for n in range(*owed_chunk(g, cols)):
-                totals[0, 1 + n] += owed[n]
+        for n in range(TILE - 1, cols - TILE + 1):
+            owed[n] = jnp.zeros((8, slots), jnp.float32)
         for n, col in enumerate(seams):
             totals[0, 1 + col] += seam_in[n]
         for g in range(groups):
@@ -646,8 +680,6 @@
         for k, g in enumerate(order):
             if k > 1:
                 arrive(("owed", g))
-            for n in range(*owed_chunk(g, cols)):
-                totals[0, 1 + n] += jnp.where(has[-1, 0], owed[n], 0.0)
             if k > 1:
                 step_group(0, g - 1, left_back)
         step_group(0, groups - 2, left_back)
@@ -655,8 +687,7 @@
         arrive("forward")
         landed[0, 0:components, :] = msg_in[0, 0:components, :]
 
-    put(0, 0, has[-1, 0], landed[0])
-    sent(*moves)
+    put(0, has[-1, 0], landed[0], lists_first)
 
 
 def body(blades, spans, fars, particles, filled, contact_pairs, contact_count, movers_out, movers_in, move_count):

time: 14.7 us -> 14.2 us (0.966)
  Pallas kernels: 13.7 us -> 13.3 us
    pallas_call x1, Pallas kernels: 13.7 us -> 13.3 us  [body(): pl.pallas_call(functools.partial(kernel, particles.shape, blades, spans,...]
where the time goes in v4:
time: 14.2 us; the launch traced here: 14.1 us
  Pallas kernels  13.3 us (94%)
  local copies, waits for them, and re-layouts  0.74 us (5%)
    pallas_call x1, Pallas kernels, body(): pl.pallas_call(functools.partial(kernel, particles.shape, blades, spans,...  13.3 us
    unnamed x1, local copies, waits for them, and re-layouts  0.74 us

profile of v4, /device:TPU:17, one launch (start us, length us, event | category | flops | bytes accessed | tf_op | source)
XLA Modules:
  0.0 14.1 jit_solution(12250279061644062130)
XLA Ops:
  0.0 13.3 %shard_map.73 = f32[11,2,32,128]{3,2,1,0:T(8,128)S(1)} custom-call(f32[11,2,32,128]{3,2,1,0:T(8,128)} %parts_hbm.1, s32[2,32]{1,0:T(2,128)} %filled_hbm.1, s32[2,2,32,128]{3,2,1,0:T(8,128)} %pairs_hbm.1, s32[2,32]{1,0:T(2,128)} %count_hbm.1, s32[2,2,1,16]{3,2,1,0:T(1,128)} %out_movers_hbm.1, s32[2,2,1,16]{3,2,1,0:T(1,128)} %in_movers_hbm.1, s32[1,1,2]{2,1,0:T(1,128)} %bitcast.1), custom_call_target="tpu_custom_call" | custom-call | tf_op jit(solution)/shard_map/pallas_call | solution.py:700
  13.3 0.7 %copy.9 = f32[11,2,32,128]{3,2,1,0:T(8,128)} copy(f32[11,2,32,128]{3,2,1,0:T(8,128)S(1)} %shard_map.73) | data formatting | bytes 720896

commit v5 on v4

--- a/solution.py
+++ b/solution.py
@@ -541,8 +541,12 @@
         pack(last, packed_last)
 
     pl.semaphore_wait(barrier, expected)
-    start("side right", "side left", ("ghost", 0), "corner left", "corner right")
-    start(*(("ghost", g) for g in order[1:]))
+    start("side right", "side left", ("ghost", 0), "corner left", ("ghost", groups - 1), "corner right")
+
+    @pl.when(~far_down)
+    def _():
+        start(*(("ghost", g) for g in middle))
+
     start("far pairs", "far count")
     for n, copy in enumerate(own):
         if n not in (0, 4):
@@ -566,7 +570,13 @@
 
     lax.fori_loop(1, groups - 1, inner, 0)
     arrive("side right", "side left")
-    lax.fori_loop(0, 2, outer, 0)
+    lax.fori_loop(0, 1, outer, 0)
+
+    @pl.when(far_down)
+    def _():
+        start(*(("ghost", g) for g in middle))
+
+    lax.fori_loop(1, 2, outer, 0)
     for r in range(rows):
         edge_out[0, r] = totals[r, 0]
         edge_out[1, r] = totals[r, wide - 1]

time: 14.2 us -> 13.8 us (0.972)
  Pallas kernels: 13.3 us -> 13 us
    pallas_call x1, Pallas kernels: 13.3 us -> 13 us  [body(): pl.pallas_call(functools.partial(kernel, particles.shape, blades, spans,...]
where the time goes in v5:
time: 13.8 us; the launch traced here: 13.7 us
  Pallas kernels  13 us (94%)
  local copies, waits for them, and re-layouts  0.74 us (5%)
    pallas_call x1, Pallas kernels, body(): pl.pallas_call(functools.partial(kernel, particles.shape, blades, spans,...  13 us
    unnamed x1, local copies, waits for them, and re-layouts  0.74 us

profile of v5, /device:TPU:17, one launch (start us, length us, event | category | flops | bytes accessed | tf_op | source)
XLA Modules:
  0.0 13.7 jit_solution(8480615853286325890)
XLA Ops:
  0.0 13.0 %shard_map.73 = f32[11,2,32,128]{3,2,1,0:T(8,128)S(1)} custom-call(f32[11,2,32,128]{3,2,1,0:T(8,128)} %parts_hbm.1, s32[2,32]{1,0:T(2,128)} %filled_hbm.1, s32[2,2,32,128]{3,2,1,0:T(8,128)} %pairs_hbm.1, s32[2,32]{1,0:T(2,128)} %count_hbm.1, s32[2,2,1,16]{3,2,1,0:T(1,128)} %out_movers_hbm.1, s32[2,2,1,16]{3,2,1,0:T(1,128)} %in_movers_hbm.1, s32[1,1,2]{2,1,0:T(1,128)} %bitcast.1), custom_call_target="tpu_custom_call" | custom-call | tf_op jit(solution)/shard_map/pallas_call | solution.py:710
  13.0 0.7 %copy.9 = f32[11,2,32,128]{3,2,1,0:T(8,128)} copy(f32[11,2,32,128]{3,2,1,0:T(8,128)S(1)} %shard_map.73) | data formatting | bytes 720896

commit v6 on v5

--- a/solution.py
+++ b/solution.py
@@ -84,11 +84,14 @@
     return g * TILE - 1, ((g + 1) * TILE - 1 if g < groups - 2 else cols - TILE + 1)
 
 
-def packing(components, slots, movers):
+def packing(components, slots, movers, groups):
     live = slots - 2 * movers
     spare = slots - live
     pieces = live // spare
     riders = components // (pieces + 1) if live % spare == 0 else 0
+    extra = (riders + 1) * pieces - (components - riders - 1)
+    if riders and extra == 1 and spare * groups <= slots:
+        riders += 1
     sent_rows = 6 if live % spare == 0 and pieces <= 6 else 8
     return live, spare, pieces, riders, sent_rows
 
@@ -130,6 +133,9 @@
     ghost,
     packed,
     packed_last,
+    rest_out,
+    rest_in,
+    rest,
     pairs_ref,
     count_own,
     count_prev,
@@ -162,8 +168,9 @@
     movers = out_movers.shape[3]
     wide = cols + 2
     groups = cols // TILE
-    live_slots, spare, pieces, riders, sent_rows = packing(components, slots, movers)
+    live_slots, spare, pieces, riders, sent_rows = packing(components, slots, movers, groups)
     carried = components - riders
+    has_rest = riders * pieces > carried
     order = order_of(cols)
     middle = order[2:]
     seams = (TILE - 1, TILE, cols - TILE - 1, cols - TILE)
@@ -251,6 +258,8 @@
     move("diag low", totals.at[rows, wide - 1], owed_diag.at[0], 1, 1)
     move("diag high", totals.at[rows, 0], owed_diag.at[1], 1, -1)
     move("seams", seam_out, seam_in, 1, 0, True)
+    move("rest", rest_out.at[0], rest_in.at[0], -1, 0)
+    move("far rest", rest_out.at[1], rest_in.at[1], 1, 0, True)
     inner_cols = slice(TILE, cols - TILE)
     target = pairs_ref.at[:, rows, inner_cols]
     move("far pairs", pairs_hbm.at[:, rows - 1, inner_cols], target, 1, 0, True)
@@ -309,20 +318,36 @@
     def pack(r, target):
         for c in range(carried):
             value = ghost[c, r, own_cols, :]
-            if c < riders * pieces:
+            if c < riders * pieces and c < carried:
                 rider, piece = carried + c // pieces, c % pieces
                 shift = live_slots - piece * spare
                 moved = pltpu.roll(ghost[rider, r, own_cols, :], shift, 1)
                 value = jnp.where(lane_ids < live_slots, value, moved)
             target[c] = value
+        if has_rest:
+            which = 0 if r == 0 else 1
+            value = None
+            for k in range(groups):
+                piece = ghost[components - 1, r, TILE + k * TILE : 2 * TILE + k * TILE, :]
+                moved = pltpu.roll(piece, (k * spare - (pieces - 1) * spare) % slots, 1)
+                value = moved if k == 0 else jnp.where(lane >= k * spare, moved, value)
+            rest_out[which] = value
+
+    def expand(which):
+        for k in range(groups):
+            shift = ((pieces - 1) * spare - k * spare) % slots
+            rest[which, k * TILE : (k + 1) * TILE] = pltpu.roll(rest_in[which], shift, 1)
 
     def unpack(r, at):
         for e in range(riders):
             value = None
             for piece in range(pieces):
                 shift = (piece * spare - live_slots) % slots
-                tile = ghost[e * pieces + piece, r, TILE + at : 2 * TILE + at, :]
-                moved = pltpu.roll(tile, shift, 1)
+                if e * pieces + piece < carried:
+                    tile = ghost[e * pieces + piece, r, TILE + at : 2 * TILE + at, :]
+                    moved = pltpu.roll(tile, shift, 1)
+                else:
+                    moved = rest[0 if r == rows else 1, at : at + TILE]
                 value = moved if piece == 0 else jnp.where(lane >= piece * spare, moved, value)
             ghost[carried + e, r, TILE + at : 2 * TILE + at, :] = value
 
@@ -541,13 +566,15 @@
         pack(last, packed_last)
 
     pl.semaphore_wait(barrier, expected)
-    start("side right", "side left", ("ghost", 0), "corner left", ("ghost", groups - 1), "corner right")
+    rest_out_used = ("rest",) if has_rest else ()
+    start(*rest_out_used, ("ghost", 0), "corner left", ("ghost", groups - 1), "corner right", "side right", "side left")
 
     @pl.when(~far_down)
     def _():
         start(*(("ghost", g) for g in middle))
 
-    start("far pairs", "far count")
+    far_rest_used = ("far rest",) if has_rest else ()
+    start("far pairs", "far count", *far_rest_used)
     for n, copy in enumerate(own):
         if n not in (0, 4):
             copy.wait()
@@ -594,6 +621,18 @@
     start(*(("far", g) for g in middle))
     lists_first, lists_last = landing_of(0, 0), landing_of(1, last)
 
+    @pl.when(far_up)
+    def _():
+        msg_out[0, 7:8, :] = cells_on.astype(jnp.float32)
+        msg_out[0, 8:9, :] = slots_on.astype(jnp.float32)
+        for c in range(components):
+            msg_out[0, 9 + c : 10 + c, :] = lines_on(ghost[c, last, own_cols, :])
+
+    @pl.when(far_down)
+    def _():
+        for n in range(TILE - 1, cols - TILE + 1):
+            owed[n] = jnp.zeros((8, slots), jnp.float32)
+
     for r in range(1, last):
         for g in range(groups):
             step_group(r, g)
@@ -601,6 +640,9 @@
     def last_group(g):
         arrive(("ghost", g))
         if g == 0:
+            if has_rest:
+                arrive("rest")
+                expand(0)
             unpack(rows, 0)
             unpack(rows, 1)
             arrive("corner left")
@@ -624,9 +666,8 @@
         for n, col in enumerate(seams):
             seam_out[n] = totals[rows, 1 + col]
         start("seams")
-        share_of(0, last, lines_on, cells_on, slots_on)
-        for c in range(components):
-            msg_out[0, 9 + c : 10 + c, :] = lines_on(ghost[c, last, own_cols, :])
+        for c in range(7):
+            msg_out[0, c : c + 1, :] = lines_on(totals[last, 1 : 1 + cols, c, :])
         start("forward")
 
     for g in middle:
@@ -657,7 +698,7 @@
         finish(1, msg_in[1], rows, late_edges, lambda c, lines: lines(ghost[c, rows, own_cols, :]))
         put(last, has[1, 0], landed[1], lists_last)
 
-    sent(*moves)
+    sent(*(w for w in moves if has_rest or w not in ("rest", "far rest")))
 
     def add_diagonals():
         totals[0, 1] += jnp.where(has[-1, -1], owed_diag[0], 0.0)
@@ -665,7 +706,9 @@
 
     @pl.when(far_down)
     def _():
-        arrive("far count", "far pairs")
+        arrive("far count", "far pairs", *far_rest_used)
+        if has_rest:
+            expand(1)
         spread(count_prev, last, count_wide, rows)
         for g in middle:
             arrive(("far", g))
@@ -673,8 +716,6 @@
             group_of(before, g, across)
         arrive(("owed", 0), ("owed", groups - 1), "seams", "diag low", "diag high")
         add_diagonals()
-        for n in range(TILE - 1, cols - TILE + 1):
-            owed[n] = jnp.zeros((8, slots), jnp.float32)
         for n, col in enumerate(seams):
             totals[0, 1 + col] += seam_in[n]
         for g in range(groups):
@@ -705,8 +746,8 @@
     padded = -(-components // 8) * 8
     message = -(-(components + 9) // 8) * 8
     f32, i32 = jnp.float32, jnp.int32
-    riders = packing(components, slots, movers_out.shape[3])[3]
-    remote_copies = 3 * (cols // TILE) + 13
+    riders = packing(components, slots, movers_out.shape[3], cols // TILE)[3]
+    remote_copies = 3 * (cols // TILE) + 15
     return pl.pallas_call(
         functools.partial(kernel, particles.shape, blades, spans, fars),
         out_shape=pltpu.VMEM(particles.shape, f32),
@@ -716,6 +757,9 @@
             pltpu.VMEM((components, rows + 2, cols + 2 * TILE, slots), f32),
             pltpu.VMEM((components - riders, cols, slots), f32),
             pltpu.VMEM((components - riders, cols, slots), f32),
+            pltpu.VMEM((2, TILE, slots), f32),
+            pltpu.VMEM((2, TILE, slots), f32),
+            pltpu.VMEM((2, cols, slots), f32),
             pltpu.VMEM((2, rows + 1, cols, contact_pairs.shape[3]), i32),
             pltpu.VMEM((rows, cols), i32),
             pltpu.VMEM((rows, cols), i32),

time: 13.8 us -> 13.8 us (level)
  no operation moved by 1% of the time
where the time goes in v6:
time: 13.8 us; the launch traced here: 13.7 us
  Pallas kernels  12.9 us (93%)
  local copies, waits for them, and re-layouts  0.74 us (5%)
    pallas_call x1, Pallas kernels, body(): pl.pallas_call(functools.partial(kernel, particles.shape, blades, spans,...  12.9 us
    unnamed x1, local copies, waits for them, and re-layouts  0.74 us

profile of v6, /device:TPU:17, one launch (start us, length us, event | category | flops | bytes accessed | tf_op | source)
XLA Modules:
  0.0 13.7 jit_solution(15000411679036331487)
XLA Ops:
  0.0 12.9 %shard_map.73 = f32[11,2,32,128]{3,2,1,0:T(8,128)S(1)} custom-call(f32[11,2,32,128]{3,2,1,0:T(8,128)} %parts_hbm.1, s32[2,32]{1,0:T(2,128)} %filled_hbm.1, s32[2,2,32,128]{3,2,1,0:T(8,128)} %pairs_hbm.1, s32[2,32]{1,0:T(2,128)} %count_hbm.1, s32[2,2,1,16]{3,2,1,0:T(1,128)} %out_movers_hbm.1, s32[2,2,1,16]{3,2,1,0:T(1,128)} %in_movers_hbm.1, s32[1,1,2]{2,1,0:T(1,128)} %bitcast.1), custom_call_target="tpu_custom_call" | custom-call | tf_op jit(solution)/shard_map/pallas_call | solution.py:751
  12.9 0.7 %copy.9 = f32[11,2,32,128]{3,2,1,0:T(8,128)} copy(f32[11,2,32,128]{3,2,1,0:T(8,128)S(1)} %shard_map.73) | data formatting | bytes 720896

commit v7 on v6

--- a/solution.py
+++ b/solution.py
@@ -613,12 +613,12 @@
     cells_on, slots_on = list_of(0, last)
     lines_on, left_on = chosen_of(cells_on, slots_on)
     arrive("edge low", "edge high")
+    start(*(("far", g) for g in middle))
     for r in range(rows):
         totals[r, 1] += jnp.where(has[0, -1], owed_low[r], 0.0)
         totals[r, cols] += jnp.where(has[0, 1], owed_high[r], 0.0)
     share_of(1, 0, lines_back, cells_back, slots_back)
     start("backward")
-    start(*(("far", g) for g in middle))
     lists_first, lists_last = landing_of(0, 0), landing_of(1, last)
 
     @pl.when(far_up)
@@ -657,9 +657,9 @@
         start(("owed", g))
 
     last_group(0)
-    start("late high", "diag high")
+    start("diag high")
     last_group(groups - 1)
-    start("late low", "diag low")
+    start("diag low")
 
     @pl.when(far_up)
     def _():
@@ -670,6 +670,7 @@
             msg_out[0, c : c + 1, :] = lines_on(totals[last, 1 : 1 + cols, c, :])
         start("forward")
 
+    start("late low", "late high")
     for g in middle:
         last_group(g)
     for g in range(groups):

time: 13.8 us -> 13.8 us (level)
  no operation moved by 1% of the time
where the time goes in v7:
time: 13.8 us; the launch traced here: 13.7 us
  Pallas kernels  12.9 us (93%)
  local copies, waits for them, and re-layouts  0.74 us (5%)
    pallas_call x1, Pallas kernels, body(): pl.pallas_call(functools.partial(kernel, particles.shape, blades, spans,...  12.9 us
    unnamed x1, local copies, waits for them, and re-layouts  0.74 us

profile of v7, /device:TPU:17, one launch (start us, length us, event | category | flops | bytes accessed | tf_op | source)
XLA Modules:
  0.0 13.7 jit_solution(3526598235420624789)
XLA Ops:
  0.0 12.9 %shard_map.73 = f32[11,2,32,128]{3,2,1,0:T(8,128)S(1)} custom-call(f32[11,2,32,128]{3,2,1,0:T(8,128)} %parts_hbm.1, s32[2,32]{1,0:T(2,128)} %filled_hbm.1, s32[2,2,32,128]{3,2,1,0:T(8,128)} %pairs_hbm.1, s32[2,32]{1,0:T(2,128)} %count_hbm.1, s32[2,2,1,16]{3,2,1,0:T(1,128)} %out_movers_hbm.1, s32[2,2,1,16]{3,2,1,0:T(1,128)} %in_movers_hbm.1, s32[1,1,2]{2,1,0:T(1,128)} %bitcast.1), custom_call_target="tpu_custom_call" | custom-call | tf_op jit(solution)/shard_map/pallas_call | solution.py:752
  12.9 0.7 %copy.9 = f32[11,2,32,128]{3,2,1,0:T(8,128)} copy(f32[11,2,32,128]{3,2,1,0:T(8,128)S(1)} %shard_map.73) | data formatting | bytes 720896
